TPU v7x, 32 devices: a whole 2x2x4 slice. The times are simulated.
32 devices in a mesh: dp: 8 (over z, x), expert: 4 (over y, core).
Axes of the slice: x: 2, y: 2, z: 4, core: 2. Of those that a mesh axis runs over, the one named last changes fastest.
Arguments:
- tokens: bfloat16 [1024, 4096], P('expert', 'dp'), may hold values from -6 to 6
- cotangent: bfloat16 [1024, 4096], P('expert', 'dp'), may hold values from -6 to 6
- expert_ids: int32 [1024, 2], P('expert'), may hold values from 0 to 3, all different within a row; in each aligned block of 256 rows (0 to 255, 256 to 511, ...) at most 129 rows name the same one
- combine: float32 [1024, 2], P('expert'), may hold values from 0.1 to 1
- w_gate: bfloat16 [4, 4096, 14336], P('expert', None, 'dp'), may hold values from -0.09375 to 0.09375
- w_up: bfloat16 [4, 4096, 14336], P('expert', None, 'dp'), may hold values from -0.09375 to 0.09375
- w_down: bfloat16 [4, 14336, 4096], P('expert', 'dp'), may hold values from -0.046875 to 0.046875
- scale_vector: float32 [4, 14336], P('expert', 'dp'), may hold values from 0.25 to 1.75
Outputs:
- token_grads: bfloat16 [1024, 4096], P('expert', 'dp')
- scale_grads: float32 [4, 14336], P('expert', 'dp')
Inputs may be any that keep to these rules, and one draw needn't show every extreme that they name: `expert_ids`: each row names 2 different experts. Among the 256 rows of one aligned block no expert is named more than 129 times, and some block names some expert exactly 129 times.
All inputs are finite; a program needn't handle non-finite values.
Results may differ from a plain program's by a relative error of at most 0.0065.
Values may be sent and summed in bfloat16 or wider, within the bound.
A program may use at most 128 MiB of HBM per device.

v0:
```python
import functools

import jax
import jax.numpy as jnp
from jax import lax
from jax.experimental import pallas as pl
from jax.experimental.pallas import tpu as pltpu
from jax.sharding import PartitionSpec as P


def route_tables(expert_ids, combine, experts, capacity):
    blocks = expert_ids.shape[0]
    per_block = expert_ids.shape[1]
    onehot = (expert_ids[:, :, :, None] == jnp.arange(experts, dtype=jnp.int32)).astype(jnp.int32)
    flat_hits = onehot.reshape(blocks, per_block * 2, experts)
    earlier = jnp.cumsum(flat_hits, axis=1) - flat_hits
    slot_ids = jnp.sum(earlier * flat_hits, axis=2).reshape(blocks, per_block, 2)
    positions = (slot_ids[:, :, :, None] == jnp.arange(capacity, dtype=jnp.int32)).astype(
        jnp.float32
    )
    matches = onehot.astype(jnp.float32)[:, :, :, :, None] * positions[:, :, :, None, :]
    dispatch = jnp.transpose(jnp.sum(matches, axis=2), (0, 2, 3, 1))
    slot_weight = jnp.sum(matches * combine[:, :, :, None, None], axis=(1, 2))
    return (dispatch, slot_weight, slot_ids)


def combine_slots(slot_table, flat_index):
    tok_count = flat_index.shape[0]
    picked = jnp.take(slot_table, flat_index.reshape(-1), axis=0).reshape(
        tok_count, 2, slot_table.shape[1]
    )
    return picked[:, 0].astype(jnp.float32) + picked[:, 1].astype(jnp.float32)


MESH = pl.DeviceIdType.MESH
ROW_TILE = 16
SHORT_RING = 8
VMEM_LIMIT = 60 * 1024 * 1024


def ring_order(mesh):
    count = mesh.shape["dp"]
    devices = mesh.devices.reshape(count, -1)[:, 0]
    places = {}
    for index, device in enumerate(devices):
        coords = getattr(device, "coords", None)
        if coords is None:
            return tuple(range(count))
        places[(coords[2], coords[0])] = index
    zs = sorted({z for z, _ in places})
    xs = sorted({x for _, x in places})
    if len(places) != count or len(zs) * len(xs) != count or len(zs) % 2 or len(xs) < 2:
        return tuple(range(count))
    order = [places[(z, xs[0])] for z in zs]
    for turn, z in enumerate(reversed(zs)):
        order += [places[(z, x)] for x in (xs[1:] if turn % 2 == 0 else xs[:0:-1])]
    return tuple(order)


def lookup(table, key):
    found = jnp.int32(table[0])
    for index in range(1, len(table)):
        found = jnp.where(key == index, jnp.int32(table[index]), found)
    return found


def ring_place(ring):
    n = len(ring)
    position_of = [0] * n
    for position, index in enumerate(ring):
        position_of[index] = position
    position = lookup(position_of, lax.axis_index("dp"))
    right = lookup(ring, lax.rem(position + 1, n))
    left = lookup(ring, lax.rem(position + n - 1, n))
    return position, right, left


def greet(right, left):
    barrier = pltpu.get_barrier_semaphore()
    for neighbour in (left, right):
        pl.semaphore_signal(barrier, inc=1, device_id={"dp": neighbour}, device_id_type=MESH)
    pl.semaphore_wait(barrier, 2)


def gather_kernel(
    ring, tile, x_ref, gate_w, up_w, gate_ref, up_ref, grads_ref, rows_ref, w_buf, w_sem, own_sem,
    send_sem, recv_sem,
):
    n = len(ring)
    width = x_ref.shape[1] // 2
    rows = x_ref.shape[0]
    cut = rows // 2 // ROW_TILE * ROW_TILE
    tiles = gate_w.shape[1] // tile
    position, right, left = ring_place(ring)
    me = lax.axis_index("dp")
    halves = (pl.ds(0, cut), pl.ds(cut, rows - cut))

    def tile_columns(t):
        return pl.ds(0, tile) if tiles == 1 else pl.ds(pl.multiple_of(t * tile, tile), tile)

    def load(t, slot):
        columns = tile_columns(t)
        return (
            pltpu.make_async_copy(gate_w.at[:, columns], w_buf.at[slot, 0], w_sem.at[slot, 0]),
            pltpu.make_async_copy(up_w.at[:, columns], w_buf.at[slot, 1], w_sem.at[slot, 1]),
        )

    for copy in load(0, 0):
        copy.start()

    def columns_of(index):
        return pl.ds(pl.multiple_of(index * width, width), width)

    for which, full in enumerate((rows_ref, grads_ref)):
        own = pltpu.make_async_copy(
            x_ref.at[:, pl.ds(which * width, width)], full.at[:, columns_of(me)], own_sem.at[which]
        )
        own.start()
        own.wait()
    greet(right, left)

    def hop(which, step, way):
        full = (rows_ref, grads_ref)[which]
        shift = n - step if way == 0 else step
        origin = lookup(ring, lax.rem(position + shift, n))
        spot = full.at[halves[way], columns_of(origin)]
        return pltpu.make_async_remote_copy(
            src_ref=spot,
            dst_ref=spot,
            send_sem=send_sem.at[which, way, step],
            recv_sem=recv_sem.at[which, way, step],
            device_id={"dp": right if way == 0 else left},
            device_id_type=MESH,
        )

    def advance(which, step):
        for way in range(2):

            @pl.when(step > 0)
            def _():
                hop(which, step - 1, way).wait_recv()

            hop(which, step, way).start()

    def rows_step(step, carry):
        advance(0, step)
        return carry

    lax.fori_loop(0, n - 1, rows_step, 0)
    for way in range(2):
        hop(1, 0, way).start()
    for way in range(2):
        hop(0, n - 2, way).wait_recv()

    def grads_step(step, carry):
        @pl.when(step > 0)
        def _():
            advance(1, step)

        @pl.when(step < tiles)
        def _():
            slot = lax.rem(step, 2)

            @pl.when(step + 1 < tiles)
            def _():
                for copy in load(step + 1, lax.rem(step + 1, 2)):
                    copy.start()

            columns = tile_columns(step)
            for copy in load(step, slot):
                copy.wait()
            gate_ref[:, columns] = jnp.dot(
                rows_ref[...], w_buf[slot, 0], preferred_element_type=jnp.float32
            )
            up_ref[:, columns] = jnp.dot(
                rows_ref[...], w_buf[slot, 1], preferred_element_type=jnp.float32
            )

        return carry

    lax.fori_loop(0, n - 1, grads_step, 0)
    for way in range(2):
        hop(1, n - 2, way).wait_recv()

    def finish(step, carry):
        for which in range(2):
            for way in range(2):
                hop(which, step, way).wait_send()
        return carry

    lax.fori_loop(0, n - 1, finish, 0)


def gather_acts(ring, x, gate_w, up_w):
    n = len(ring)
    rows, width = x.shape[0], x.shape[1] // 2
    hidden = gate_w.shape[1]
    tile = 256 if hidden % 256 == 0 and hidden // 256 <= n - 1 else hidden
    full = n * width
    vmem = pl.BlockSpec(memory_space=pltpu.VMEM)
    anywhere = pl.BlockSpec(memory_space=pl.ANY)
    return pl.pallas_call(
        functools.partial(gather_kernel, ring, tile),
        out_shape=(
            jax.ShapeDtypeStruct((rows, hidden), jnp.float32),
            jax.ShapeDtypeStruct((rows, hidden), jnp.float32),
            jax.ShapeDtypeStruct((rows, full), jnp.bfloat16),
        ),
        in_specs=[anywhere, anywhere, anywhere],
        out_specs=(vmem, vmem, vmem),
        scratch_shapes=[
            pltpu.VMEM((rows, full), jnp.bfloat16),
            pltpu.VMEM((2, 2, full, tile), jnp.bfloat16),
            pltpu.SemaphoreType.DMA((2, 2)),
            pltpu.SemaphoreType.DMA((2,)),
            pltpu.SemaphoreType.DMA((2, 2, n - 1)),
            pltpu.SemaphoreType.DMA((2, 2, n - 1)),
        ],
        compiler_params=pltpu.CompilerParams(
            collective_id=0, has_side_effects=True, vmem_limit_bytes=VMEM_LIMIT
        ),
    )(x, gate_w, up_w)


def scatter_kernel(
    ring, gate_grad, up_grad, gate_w, up_w, out_ref, buf, w_buf, w_sem, send_sem, recv_sem
):
    n = len(ring)
    half = buf.shape[3]
    position, right, left = ring_place(ring)

    def load(step, slot):
        copies = []
        for way in range(2):
            shift = 2 * n - 1 - step if way == 0 else 1 + step
            owner = lookup(ring, lax.rem(position + shift, n))
            lines = pl.ds(pl.multiple_of(owner * (2 * half) + way * half, half), half)
            for kind, weight in enumerate((gate_w, up_w)):
                copies.append(
                    pltpu.make_async_copy(
                        weight.at[lines, :], w_buf.at[slot, way, kind], w_sem.at[slot, way, kind]
                    )
                )
        return copies

    for copy in load(0, 0):
        copy.start()
    greet(right, left)

    def hop(step, way):
        return pltpu.make_async_remote_copy(
            src_ref=buf.at[way, step],
            dst_ref=buf.at[way, step + 1],
            send_sem=send_sem.at[way, step],
            recv_sem=recv_sem.at[way, step],
            device_id={"dp": right if way == 0 else left},
            device_id_type=MESH,
        )

    def product(slot, way):
        across = (((1,), (1,)), ((), ()))
        return lax.dot_general(
            gate_grad[...], w_buf[slot, way, 0], across, preferred_element_type=jnp.float32
        ) + lax.dot_general(
            up_grad[...], w_buf[slot, way, 1], across, preferred_element_type=jnp.float32
        )

    def one_step(step, carry):
        slot = lax.rem(step, 2)

        @pl.when(step + 1 < n)
        def _():
            for copy in load(step + 1, lax.rem(step + 1, 2)):
                copy.start()

        for copy in load(step, slot):
            copy.wait()
        for way in range(2):
            part = product(slot, way)

            @pl.when(step == 0)
            def _():
                buf[way, 0] = part.astype(buf.dtype)

            @pl.when(step > 0)
            def _():
                hop(step - 1, way).wait_recv()
                total = buf[way, step].astype(jnp.float32) + part

                @pl.when(step < n - 1)
                def _():
                    buf[way, step] = total.astype(buf.dtype)

                @pl.when(step == n - 1)
                def _():
                    out_ref[way] = total.astype(out_ref.dtype)

            @pl.when(step < n - 1)
            def _():
                hop(step, way).start()

        return carry

    lax.fori_loop(0, n, one_step, 0)

    def finish(step, carry):
        for way in range(2):
            hop(step, way).wait_send()
        return carry

    lax.fori_loop(0, n - 1, finish, 0)


def scatter_rows(ring, gate_grad, up_grad, gate_w, up_w):
    n = len(ring)
    rows, hidden = gate_grad.shape
    half = gate_w.shape[0] // n // 2
    wire = jnp.bfloat16 if n <= SHORT_RING else jnp.float32
    vmem = pl.BlockSpec(memory_space=pltpu.VMEM)
    anywhere = pl.BlockSpec(memory_space=pl.ANY)
    return pl.pallas_call(
        functools.partial(scatter_kernel, ring),
        out_shape=jax.ShapeDtypeStruct((2, rows, half), wire),
        in_specs=[vmem, vmem, anywhere, anywhere],
        out_specs=vmem,
        scratch_shapes=[
            pltpu.VMEM((2, n, rows, half), wire),
            pltpu.VMEM((2, 2, 2, half, hidden), jnp.bfloat16),
            pltpu.SemaphoreType.DMA((2, 2, 2)),
            pltpu.SemaphoreType.DMA((2, n - 1)),
            pltpu.SemaphoreType.DMA((2, n - 1)),
        ],
        compiler_params=pltpu.CompilerParams(
            collective_id=1, has_side_effects=True, vmem_limit_bytes=VMEM_LIMIT
        ),
    )(gate_grad, up_grad, gate_w, up_w)


def local(ring, tokens, cotangent, expert_ids, combine, w_gate, w_up, w_down, scale_vector):
    experts = lax.axis_size("expert")
    tok_count = tokens.shape[0]
    capacity = 2 * tok_count // experts + 1
    dispatch, slot_weight, slot_ids = route_tables(
        expert_ids[None], combine[None], experts, capacity
    )
    dispatch_half = dispatch[0].astype(jnp.bfloat16)
    slot_weight = slot_weight[0]
    flat_index = expert_ids * capacity + slot_ids[0]
    sent_rows = jnp.einsum(
        "ect,td->ecd", dispatch_half, tokens, preferred_element_type=jnp.float32
    ).astype(jnp.bfloat16)
    cot_rows = jnp.einsum(
        "ect,td->ecd", dispatch_half, cotangent, preferred_element_type=jnp.float32
    )
    sent_grads = (slot_weight[:, :, None] * cot_rows).astype(jnp.bfloat16)
    sent = jnp.concatenate([sent_rows, sent_grads], axis=2)
    got = lax.all_to_all(sent, "expert", split_axis=0, concat_axis=0, tiled=True)
    row_count = experts * capacity
    padding = -row_count % ROW_TILE
    x = jnp.pad(got.reshape(row_count, got.shape[2]), ((0, padding), (0, 0)))
    gate_w = w_gate[0]
    up_w = w_up[0]
    down_w = w_down[0]
    gate_act, up_act, grads = gather_acts(ring, x, gate_w, up_w)
    hidden_grad = lax.dot_general(
        grads, down_w, (((1,), (1,)), ((), ())), preferred_element_type=jnp.float32
    )
    sigmoid_gate = jax.nn.sigmoid(gate_act)
    silu_gate = gate_act * sigmoid_gate
    scale_grad = jnp.sum(hidden_grad * silu_gate * up_act, axis=0)
    scaled_grad = hidden_grad * scale_vector[0]
    up_grad = (scaled_grad * silu_gate).astype(jnp.bfloat16)
    gate_grad = (
        scaled_grad * up_act * sigmoid_gate * (1.0 + gate_act * (1.0 - sigmoid_gate))
    ).astype(jnp.bfloat16)
    halves = scatter_rows(ring, gate_grad, up_grad, gate_w, up_w)
    summed = jnp.concatenate([halves[0], halves[1]], axis=1)[:row_count]
    slot_part = summed.reshape(experts, capacity, summed.shape[1])
    returned = lax.all_to_all(slot_part, "expert", split_axis=0, concat_axis=0, tiled=True)
    token_grads = combine_slots(returned.reshape(row_count, returned.shape[2]), flat_index)
    return (token_grads.astype(jnp.bfloat16), scale_grad[None, :])


def solution(mesh):
    placed = (
        P("expert", "dp"),
        P("expert", "dp"),
        P("expert", None),
        P("expert", None),
        P("expert", None, "dp"),
        P("expert", None, "dp"),
        P("expert", "dp", None),
        P("expert", "dp"),
    )
    return jax.shard_map(
        functools.partial(local, ring_order(mesh)),
        mesh=mesh,
        in_specs=placed,
        out_specs=(P("expert", "dp"), P("expert", "dp")),
        check_vma=False,
    )
```

profile of v0, /device:TPU:0, one launch (start us, length us, event | category | flops | bytes accessed | tf_op | source)
XLA Modules:
  0.0 237.0 jit_solution(15549795996586648786)
XLA Ops:
  0.6 0.0 copy-start
  0.6 0.9 copy.30
  1.5 0.1 eq.57
  1.7 1.2 reduce-window.6
  2.9 0.2 slice_reduce_fusion
  3.1 0.7 convert_convert_fusion
  3.8 0.2 reduce-window.9
  4.0 0.1 broadcast.131
  4.1 0.1 squeeze_reshape.3
  4.3 0.1 copy.31
  4.4 0.0 copy-start.3
  4.4 1.3 multiply_reduce_fusion.1
  5.8 0.1 copy.34
  5.8 0.0 copy-done
  5.8 0.3 convolution_convert_fusion
  6.2 1.3 fusion.3
  7.4 1.1 pad_maximum_fusion
  8.5 4.3 %all-to-all-start = ((bf16[4,129,1024]{2,1,0:T(8,128)(2,1)}), bf16[4,129,1024]{2,1,0:T(8,128)(2,1)S(1)}, u32[]{:S(2)}, u32[]{:S(2)}) async-start(bf16[4,129,1024]{2,1,0:T(8,128)(2,1)} %pad_maximum_fusion), calls=%async_computation | async-start | bytes 2228224 | tf_op jit(solution)/shard_map/all_to_all | solution.py:357
  12.8 0.0 copy-done.3
  12.8 15.1 %all-to-all-done = bf16[4,129,1024]{2,1,0:T(8,128)(2,1)S(1)} async-done(((bf16[4,129,1024]{2,1,0:T(8,128)(2,1)}), bf16[4,129,1024]{2,1,0:T(8,128)(2,1)S(1)}, u32[]{:S(2)}, u32[]{:S(2)}) %all-to-all-start) | async-done | bytes 1056800 | tf_op jit(solution)/shard_map/all_to_all | solution.py:357
  27.9 0.3 reshape.200
  28.2 1.1 pad.4.x_ref
  29.3 106.8 %shard_map.95 = (f32[528,1792]{1,0:T(8,128)}, f32[528,1792]{1,0:T(8,128)}, bf16[528,4096]{1,0:T(8,128)(2,1)}) custom-call(bf16[528,1024]{1,0:T(8,128)(2,1)} %pad.4.x_ref, bf16[4096,1792]{1,0:T(8,128)(2,1)} %bitcast.35, bf16[4096,1792]{1,0:T(8,128)(2,1)} %bitcast.37), custom_call_target="tpu_custom_call" | custom-call | tf_op jit(solution)/shard_map/pallas_call | solution.py:202
  136.2 18.6 %multiply_reduce_fusion = (f32[1792]{0:T(1024)S(1)}, bf16[528,1792]{1,0:T(8,128)(2,1)}, bf16[528,1792]{1,0:T(8,128)(2,1)}) fusion(f32[528,1792]{1,0:T(8,128)} %get-tuple-element.6, f32[528,1792]{1,0:T(8,128)} %get-tuple-element.7, f32[1792]{0:T(1024)S(1)} %reduce.4, bf16[528,4096]{1,0:T(8,128)(2,1)} %get-tuple-element.5, bf16[1,1792,4096]{2,1,0:T(8,128)(2,1)} %param.14), kind=kOutput, calls=%fused_computation.3 | convolution fusion | flops 7767156736 | bytes 30373888 | tf_op jit(solution)/shard_map/dot_general | solution.py:365
  154.8 64.2 %shard_map.96 = bf16[2,528,256]{2,1,0:T(8,128)(2,1)} custom-call(bf16[528,1792]{1,0:T(8,128)(2,1)} %get-tuple-element.13.gate_grad, bf16[528,1792]{1,0:T(8,128)(2,1)} %get-tuple-element.14.up_grad, bf16[4096,1792]{1,0:T(8,128)(2,1)} %bitcast.36, bf16[4096,1792]{1,0:T(8,128)(2,1)} %bitcast.38), custom_call_target="tpu_custom_call" | custom-call | tf_op jit(solution)/shard_map/pallas_call | solution.py:321
  219.0 0.0 copy-start.2
  219.1 1.1 slice_bitcast_fusion.1
  220.2 0.9 reshape.201
  221.1 3.5 %all-to-all-start.1 = ((bf16[4,129,512]{2,1,0:T(8,128)(2,1)}), bf16[4,129,512]{2,1,0:T(8,128)(2,1)S(1)}, u32[]{:S(2)}, u32[]{:S(2)}) async-start(bf16[4,129,512]{2,1,0:T(8,128)(2,1)} %reshape.201), calls=%async_computation.1 | async-start | bytes 1114112 | tf_op jit(solution)/shard_map/all_to_all | solution.py:379
  224.6 0.0 copy-done.2
  224.6 0.1 copy.36
  224.8 0.1 reshape.203
  224.9 0.6 broadcast_in_dim.19
  225.5 8.2 %all-to-all-done.1 = bf16[4,129,512]{2,1,0:T(8,128)(2,1)S(1)} async-done(((bf16[4,129,512]{2,1,0:T(8,128)(2,1)}), bf16[4,129,512]{2,1,0:T(8,128)(2,1)S(1)}, u32[]{:S(2)}, u32[]{:S(2)}) %all-to-all-start.1) | async-done | bytes 528416 | tf_op jit(solution)/shard_map/all_to_all | solution.py:379
  233.7 0.0 copy-start.1
  233.7 0.1 reshape.202
  233.9 2.0 gather_fusion
  235.9 0.2 gather.7
  236.1 0.1 copy_select_fusion
  236.2 0.8 fusion.6
  237.0 0.0 copy-done.1
  (12 shorter events, 0.2 us)
Async XLA Ops:
  0.6 5.2 %copy-start = (bf16[256,512]{1,0:T(8,128)(2,1)S(1)}, bf16[256,512]{1,0:T(8,128)(2,1)}, u32[]{:S(2)}) copy-start(bf16[256,512]{1,0:T(8,128)(2,1)} %param.8) | copy-start | bytes 786436
  4.4 8.5 %copy-start.3 = (f32[1,1792]{1,0:T(1,128)S(1)}, f32[1,1792]{1,0:T(1,128)}, u32[]{:S(2)}) copy-start(f32[1,1792]{1,0:T(1,128)} %param.15) | copy-start | bytes 21508
  8.5 19.4 %all-to-all-start = ((bf16[4,129,1024]{2,1,0:T(8,128)(2,1)}), bf16[4,129,1024]{2,1,0:T(8,128)(2,1)S(1)}, u32[]{:S(2)}, u32[]{:S(2)}) async-start(bf16[4,129,1024]{2,1,0:T(8,128)(2,1)} %pad_maximum_fusion), calls=%async_computation | async-start | bytes 2228224 | tf_op jit(solution)/shard_map/all_to_all | solution.py:357
  219.0 5.6 %copy-start.2 = (s32[256,2]{0,1:T(2,128)S(1)}, s32[256,2]{0,1:T(2,128)}, u32[]{:S(2)}) copy-start(s32[256,2]{0,1:T(2,128)} %param.10) | copy-start | bytes 6148
  221.1 12.6 %all-to-all-start.1 = ((bf16[4,129,512]{2,1,0:T(8,128)(2,1)}), bf16[4,129,512]{2,1,0:T(8,128)(2,1)S(1)}, u32[]{:S(2)}, u32[]{:S(2)}) async-start(bf16[4,129,512]{2,1,0:T(8,128)(2,1)} %reshape.201), calls=%async_computation.1 | async-start | bytes 1114112 | tf_op jit(solution)/shard_map/all_to_all | solution.py:379
  233.7 3.3 %copy-start.1 = (bf16[256,512]{1,0:T(8,128)(2,1)S(1)}, bf16[256,512]{1,0:T(8,128)(2,1)}, u32[]{:S(2)}) copy-start(bf16[256,512]{1,0:T(8,128)(2,1)} %param.8) | copy-start | bytes 786436
where the time goes:
time: 237 us
  Pallas kernels  171 us (72%)
  waiting for transfers between devices  23.3 us (10%)
  matrix products  20.2 us (9%)
  local copies, waits for them, and re-layouts  8.24 us (3%)
  starting transfers between devices  7.73 us (3%)
  other arithmetic  5.62 us (2%)
    pallas_call x1, Pallas kernels, gather_acts(): pl.pallas_call(functools.partial(gather_kernel, ring, tile), out_shape=(j...  107 us
    pallas_call x1, Pallas kernels, scatter_rows(): pl.pallas_call(functools.partial(scatter_kernel, ring), out_shape=jax.Sha...  64.2 us
    dot_general x1, matrix products, local(): lax.dot_general(grads, down_w, (((1,), (1,)), ((), ())), preferred_elemen...  18.6 us
    all_to_all x1, waiting for transfers between devices, local(): lax.all_to_all(sent, 'expert', split_axis=0, concat_axis=0, tiled=True)  15.1 us
    all_to_all x1, waiting for transfers between devices, local(): lax.all_to_all(slot_part, 'expert', split_axis=0, concat_axis=0, tiled=True)  8.19 us
  transfers between devices with their start and end apart: 2, of which 2 were waited for; matrix products, arithmetic and copies ran while one was open for 0% of the time, Pallas kernels for 0%

commit v1 on v0

--- a/solution.py
+++ b/solution.py
@@ -336,6 +336,634 @@
     )(gate_grad, up_grad, gate_w, up_w)
 
 
+PAIR = 2
+TILE = 256
+UP, DOWN, FIRST, LAST, TWIN = range(5)
+FRONT_PLAN = (
+    ("xl", 0, 0), ("xa", 0, 0), ("xb", 0, 1), ("gl", 0, 1), ("gl", 1, 1), ("xb", 1, 1),
+    ("gb", 0, 2), ("gb", 1, 2), ("cx", 0, 2), ("cx", 1, 2), ("cg", 0, 3), ("cg", 1, 3),
+)
+BACK_LAGS = (2, 3)
+
+
+def near_first(depth):
+    table = []
+    for z in range(depth):
+        low = 2 * z < depth
+        table.append(sorted(range(depth), key=lambda q: (abs(q - z), (q > z) == low)))
+    return table
+
+
+class Seat:
+    def __init__(self, depth, far):
+        self.depth = depth
+        self.dp = lax.axis_index("dp")
+        self.expert = lax.axis_index("expert")
+        self.z, self.x = lax.div(self.dp, PAIR), lax.rem(self.dp, PAIR)
+        self.y, self.core = lax.div(self.expert, PAIR), lax.rem(self.expert, PAIR)
+        table = near_first(depth)
+        self.table = [q for row in table for q in (row[::-1] if far else row)]
+        core, dp, expert = self.core, self.dp, self.expert
+        dx, dy = 1 - 2 * self.x, 2 - 4 * self.y
+        self.twin = {"dp": dp, "expert": expert + 1 - 2 * core}
+        self.across_x = {"dp": dp + dx, "expert": expert}
+        self.across_y = {"dp": dp, "expert": expert + dy}
+        self.corner = {"dp": dp, "expert": 3 - expert}
+        self.first = {"dp": dp + (1 - core) * dx, "expert": expert + core * dy}
+        self.last = {"dp": dp + core * dx, "expert": expert + (1 - core) * dy}
+        self.up = {"dp": dp + PAIR, "expert": expert}
+        self.down = {"dp": dp - PAIR, "expert": expert}
+        self.has_up = self.z < depth - 1
+        self.has_down = self.z > 0
+
+    def line(self, k):
+        return lookup(self.table, self.z * self.depth + k)
+
+    def spot(self, q, a, b):
+        core = self.core
+        across = lax.rem(self.x + a + core * (b - a), PAIR)
+        beside = lax.rem(self.y + b + core * (a - b), PAIR)
+        return q * PAIR + across, beside
+
+    def greet(self):
+        barrier = pltpu.get_barrier_semaphore()
+
+        def tell(target):
+            pl.semaphore_signal(barrier, inc=1, device_id=target, device_id_type=MESH)
+
+        for target in (self.twin, self.across_x, self.across_y, self.corner):
+            tell(target)
+
+        @pl.when(self.has_up)
+        def _():
+            tell(self.up)
+
+        @pl.when(self.has_down)
+        def _():
+            tell(self.down)
+
+        ends = jnp.where(self.has_up, 1, 0) + jnp.where(self.has_down, 1, 0)
+        pl.semaphore_wait(barrier, 4 + ends)
+
+
+def remote(source, target, send_sem, recv_sem, device):
+    return pltpu.make_async_remote_copy(
+        src_ref=source, dst_ref=target, send_sem=send_sem, recv_sem=recv_sem,
+        device_id=device, device_id_type=MESH,
+    )
+
+
+def run_plan(depth, plan, ops):
+    span = depth + max(lag for _, _, lag in plan)
+
+    def turn(i, carry):
+        for name, part, lag in plan:
+
+            @pl.when((i >= lag) & (i < lag + depth))
+            def _(name=name, part=part, lag=lag):
+                ops[name](i - lag, part)
+
+        return carry
+
+    lax.fori_loop(0, span, turn, 0)
+
+
+def front_kernel(
+    depth, main, meta_ref, x_ref, g_ref, gate_w, up_w, down_w, scale_ref, gate_ref, up_ref,
+    total_ref, back_ref, full, meta, hot, weight, rows, gate, up, hid, w_buf, d_buf, total,
+    own_sem, w_sem, d_sem, note_send, note_recv, send_sem, recv_sem,
+):
+    seat = Seat(depth, False)
+    blocks = PAIR * PAIR
+    feat = x_ref.shape[1]
+    tok = x_ref.shape[0]
+    hidden = gate.shape[1]
+    slots = hot.shape[1]
+    tile = TILE if hidden % TILE == 0 else hidden
+    z = seat.z
+
+    def shard(k, a):
+        return seat.line(k) * PAIR + lax.rem(seat.x + a, PAIR)
+
+    def load_up(k, a):
+        lines = pl.ds(pl.multiple_of(shard(k, a) * feat, feat), feat)
+        return (
+            pltpu.make_async_copy(gate_w.at[lines, :], w_buf.at[a, 0], w_sem.at[a, 0]),
+            pltpu.make_async_copy(up_w.at[lines, :], w_buf.at[a, 1], w_sem.at[a, 1]),
+        )
+
+    def load_down(k, a):
+        columns = pl.ds(pl.multiple_of(shard(k, a) * feat, feat), feat)
+        return (pltpu.make_async_copy(down_w.at[:, columns], d_buf.at[a], d_sem.at[a]),)
+
+    own = [
+        pltpu.make_async_copy(ref, full.at[t, seat.dp, seat.expert], own_sem.at[t])
+        for t, ref in enumerate((x_ref, g_ref))
+    ]
+    for copy in own:
+        copy.start()
+    meta[seat.expert] = meta_ref[...]
+    seat.greet()
+
+    def note(n, target):
+        return remote(
+            meta_ref, meta.at[seat.expert], note_send.at[n], note_recv.at[seat.expert], target
+        )
+
+    notes = [
+        note(n, target) for n, target in enumerate((seat.twin, seat.across_y, seat.corner))
+    ]
+
+    def link(t, q, a, b, kind):
+        d, beside = seat.spot(q, a, b)
+        block = beside * PAIR + seat.core
+        place = full.at[t, d, block]
+        target = (seat.up, seat.down, seat.first, seat.last, seat.twin)[kind]
+        number = q * blocks + a * PAIR + b
+        return remote(
+            place, place, send_sem.at[t, kind, number], recv_sem.at[t, d, block], target
+        )
+
+    def arrived(t, q, a, b):
+        link(t, q, a, b, TWIN).wait_recv()
+
+    def along(t, q, a, act):
+        @pl.when((q <= z) & seat.has_up)
+        def _():
+            act(link(t, q, a, 0, UP))
+
+        @pl.when((q >= z) & seat.has_down)
+        def _():
+            act(link(t, q, a, 0, DOWN))
+
+    def begin(copy):
+        copy.start()
+
+    def drain(copy):
+        copy.wait_send()
+
+    def x_line(k, _):
+        q = seat.line(k)
+
+        @pl.when(k > 0)
+        def _():
+            arrived(0, q, 0, 0)
+            along(0, q, 0, begin)
+            for kind in (FIRST, LAST, TWIN):
+                link(0, q, 0, 0, kind).start()
+
+    def x_first(k, _):
+        q = seat.line(k)
+        arrived(0, q, 1, 0)
+        link(0, q, 1, 0, LAST).start()
+        link(0, q, 1, 0, TWIN).start()
+
+    def from_last(t):
+        def op(k, a):
+            q = seat.line(k)
+            arrived(t, q, a, 1)
+            link(t, q, a, 1, TWIN).start()
+
+        return op
+
+    def g_line(k, a):
+        q = seat.line(k)
+
+        def pass_on():
+            arrived(1, q, a, 0)
+            along(1, q, a, begin)
+            link(1, q, a, 0, LAST).start()
+            link(1, q, a, 0, TWIN).start()
+
+        if a:
+            pass_on()
+        else:
+            pl.when(k > 0)(pass_on)
+
+    def dispatch(t, d):
+        for beside in range(PAIR):
+            block = beside * PAIR + 1 - seat.core
+            place = full.at[t, d, block]
+            remote(
+                place, place, send_sem.at[t, TWIN, 0], recv_sem.at[t, d, block], seat.twin
+            ).wait_recv()
+        rest = None
+        for block in range(blocks):
+            got = jnp.dot(hot[block], full[t, d, block], preferred_element_type=jnp.float32)
+            if t:
+                got = got * weight[block]
+            rows[block * main : (block + 1) * main, :] = got[:main].astype(rows.dtype)
+            rest = got[main:] if rest is None else rest + got[main:]
+        rows[blocks * main :, :] = rest.astype(rows.dtype)
+
+    def again(load, k, a):
+        @pl.when(k + 1 < depth)
+        def _():
+            for copy in load(k + 1, a):
+                copy.start()
+
+    def x_products(k, a):
+        dispatch(0, shard(k, a))
+        for copy in load_up(k, a):
+            copy.wait()
+        for which, acts in enumerate((gate, up)):
+            for n in range(0, hidden, tile):
+                columns = slice(n, n + tile)
+                acts[:, columns] += jnp.dot(
+                    rows[...], w_buf[a, which, :, columns], preferred_element_type=jnp.float32
+                )
+        again(load_up, k, a)
+
+    def g_products(k, a):
+        dispatch(1, shard(k, a))
+        for copy in load_down(k, a):
+            copy.wait()
+        for n in range(0, hidden, tile):
+            columns = slice(n, n + tile)
+            hid[:, columns] += lax.dot_general(
+                rows[...], d_buf[a, columns, :], (((1,), (1,)), ((), ())),
+                preferred_element_type=jnp.float32,
+            )
+        again(load_down, k, a)
+
+    for copy in own:
+        copy.wait()
+    for copy in notes:
+        copy.start()
+    along(0, z, 0, begin)
+    for kind in (FIRST, LAST, TWIN):
+        link(0, z, 0, 0, kind).start()
+    along(1, z, 0, begin)
+    for kind in (FIRST, LAST, TWIN):
+        link(1, z, 0, 0, kind).start()
+    for a in range(PAIR):
+        for copy in load_up(0, a) + load_down(0, a):
+            copy.start()
+    for acts in (gate, up, hid, total):
+        acts[...] = jnp.zeros_like(acts)
+
+    down_rows = lax.broadcasted_iota(jnp.int32, (tok, tok), 0)
+    over_columns = lax.broadcasted_iota(jnp.int32, (tok, tok), 1)
+    before = (down_rows < over_columns).astype(jnp.bfloat16)
+    slot_rows = lax.broadcasted_iota(jnp.int32, (slots, tok), 0).astype(jnp.float32)
+    slot_columns = lax.broadcasted_iota(jnp.int32, (tok, slots), 1).astype(jnp.float32)
+    mine = seat.expert.astype(jnp.float32)
+    for n, target in enumerate((seat.twin, seat.across_y, seat.corner)):
+        other = target["expert"]
+        remote(
+            meta_ref, meta.at[other], note_send.at[n], note_recv.at[other], target
+        ).wait_recv()
+    for block in range(blocks):
+        notes_in = meta[block]
+        named = (notes_in[0:PAIR] == mine).astype(jnp.float32)
+        hit = named[0:1] + named[1:PAIR]
+        earlier = jnp.dot(
+            jnp.broadcast_to(hit, (8, tok)).astype(jnp.bfloat16), before,
+            preferred_element_type=jnp.float32,
+        )[0:1]
+        spilled = jnp.where(earlier < main, earlier, float(main + block))
+        want = jnp.where(hit > 0, spilled, -1.0)
+        chosen = (slot_rows == want).astype(jnp.float32)
+        hot[block] = chosen.astype(hot.dtype)
+        share = named[0:1] * notes_in[PAIR : PAIR + 1] + named[1:2] * notes_in[PAIR + 1 : PAIR + 2]
+        weight[block] = jnp.sum(chosen * share, axis=1, keepdims=True)
+        want_column = jnp.sum(
+            jnp.where(down_rows == over_columns, want, 0.0), axis=1, keepdims=True
+        )
+        back_ref[block] = (slot_columns == want_column).astype(back_ref.dtype)
+
+    run_plan(
+        depth, FRONT_PLAN,
+        {
+            "xl": x_line, "xa": x_first, "xb": from_last(0), "gl": g_line, "gb": from_last(1),
+            "cx": x_products, "cg": g_products,
+        },
+    )
+
+    step = ROW_TILE
+
+    def finish(i, carry):
+        lines = pl.ds(pl.multiple_of(i * step, step), step)
+        gate_act, up_act, hidden_grad = gate[lines, :], up[lines, :], hid[lines, :]
+        sigmoid_gate = jax.nn.sigmoid(gate_act)
+        silu_gate = gate_act * sigmoid_gate
+        total[...] += hidden_grad * silu_gate * up_act
+        scaled_grad = hidden_grad * scale_ref[...]
+        up_ref[lines, :] = (scaled_grad * silu_gate).astype(up_ref.dtype)
+        gate_ref[lines, :] = (
+            scaled_grad * up_act * sigmoid_gate * (1.0 + gate_act * (1.0 - sigmoid_gate))
+        ).astype(gate_ref.dtype)
+        return carry
+
+    lax.fori_loop(0, gate.shape[0] // step, finish, 0)
+    total_ref[...] = jnp.sum(total[...], axis=0, keepdims=True)
+
+    for copy in notes:
+        copy.wait_send()
+
+    def settle(k, carry):
+        for t in range(2):
+            for a in range(PAIR):
+                if t or not a:
+                    along(t, k, a, drain)
+                for b in range(PAIR):
+                    link(t, k, a, b, TWIN).wait_send()
+                link(t, k, a, 0, LAST).wait_send()
+        link(0, k, 0, 0, FIRST).wait_send()
+        return carry
+
+    lax.fori_loop(0, depth, settle, 0)
+    link(1, z, 0, 0, FIRST).wait_send()
+
+
+def front(depth, meta, tokens, cotangent, gate_w, up_w, down_w, scale):
+    tok, feat = tokens.shape
+    hidden = gate_w.shape[1]
+    blocks = PAIR * PAIR
+    main = 2 * tok // blocks
+    slots = main + ROW_TILE
+    count = blocks * main + ROW_TILE
+    shards = depth * PAIR
+    vmem = pl.BlockSpec(memory_space=pltpu.VMEM)
+    anywhere = pl.BlockSpec(memory_space=pl.ANY)
+    half, wide = jnp.bfloat16, jnp.float32
+    dma = pltpu.SemaphoreType.DMA
+    return pl.pallas_call(
+        functools.partial(front_kernel, depth, main),
+        out_shape=(
+            jax.ShapeDtypeStruct((count, hidden), half),
+            jax.ShapeDtypeStruct((count, hidden), half),
+            jax.ShapeDtypeStruct((1, hidden), wide),
+            jax.ShapeDtypeStruct((blocks, tok, slots), half),
+        ),
+        in_specs=[vmem] + [anywhere] * 5 + [vmem],
+        out_specs=(vmem, vmem, vmem, vmem),
+        scratch_shapes=[
+            pltpu.VMEM((2, shards, blocks, tok, feat), half),
+            pltpu.VMEM((blocks,) + meta.shape, wide),
+            pltpu.VMEM((blocks, slots, tok), half),
+            pltpu.VMEM((blocks, slots, 1), wide),
+            pltpu.VMEM((count, feat), half),
+            pltpu.VMEM((count, hidden), wide),
+            pltpu.VMEM((count, hidden), wide),
+            pltpu.VMEM((count, hidden), wide),
+            pltpu.VMEM((PAIR, 2, feat, hidden), half),
+            pltpu.VMEM((PAIR, hidden, feat), half),
+            pltpu.VMEM((ROW_TILE, hidden), wide),
+            dma((2,)),
+            dma((PAIR, 2)),
+            dma((PAIR,)),
+            dma((3,)),
+            dma((blocks,)),
+            dma((2, 5, depth * blocks)),
+            dma((2, shards, blocks)),
+        ],
+        compiler_params=pltpu.CompilerParams(
+            collective_id=2, has_side_effects=True, vmem_limit_bytes=VMEM_LIMIT
+        ),
+    )(meta, tokens, cotangent, gate_w, up_w, down_w, scale)
+
+
+def back_kernel(
+    depth, main, gate_grad, up_grad, back, gate_w, up_w, out_ref, prow, kept, away, came, acc,
+    out_last, in_last, out_first, in_first, out_line, in_up, in_down, w_buf, w_sem, twin_send,
+    twin_recv, last_send, last_recv, first_send, first_recv, line_send, line_recv,
+):
+    seat = Seat(depth, True)
+    blocks = PAIR * PAIR
+    tok, feat = out_ref.shape
+    shards = depth * PAIR
+    tile = TILE if feat % TILE == 0 else feat
+    z = seat.z
+
+    def shard(s):
+        return seat.line(lax.div(s, PAIR)) * PAIR + lax.rem(seat.x + 1 + s, PAIR)
+
+    def load(s):
+        slot = lax.rem(s, 2)
+        lines = pl.ds(pl.multiple_of(shard(s) * feat, feat), feat)
+        return (
+            pltpu.make_async_copy(gate_w.at[lines, :], w_buf.at[slot, 0], w_sem.at[slot, 0]),
+            pltpu.make_async_copy(up_w.at[lines, :], w_buf.at[slot, 1], w_sem.at[slot, 1]),
+        )
+
+    for copy in load(0):
+        copy.start()
+    seat.greet()
+
+    def to_twin(d, beside):
+        return remote(
+            away.at[d, beside], came.at[d, beside], twin_send.at[d, beside],
+            twin_recv.at[d, beside], seat.twin,
+        )
+
+    def to_last(n):
+        return remote(
+            out_last.at[n], in_last.at[n], last_send.at[n], last_recv.at[n], seat.last
+        )
+
+    def to_first(q):
+        return remote(
+            out_first.at[q], in_first.at[q], first_send.at[q], first_recv.at[q], seat.first
+        )
+
+    def to_up(q):
+        return remote(
+            out_line.at[q], in_up.at[q], line_send.at[q], line_recv.at[0, q], seat.up
+        )
+
+    def to_down(q):
+        return remote(
+            out_line.at[q], in_down.at[q], line_send.at[q], line_recv.at[1, q], seat.down
+        )
+
+    def product(s):
+        slot = lax.rem(s, 2)
+
+        @pl.when(s + 1 < shards)
+        def _():
+            for copy in load(s + 1):
+                copy.start()
+
+        for copy in load(s):
+            copy.wait()
+        across = (((1,), (1,)), ((), ()))
+        for n in range(0, feat, tile):
+            columns = slice(n, n + tile)
+            part = lax.dot_general(
+                gate_grad[...], w_buf[slot, 0, columns, :], across,
+                preferred_element_type=jnp.float32,
+            ) + lax.dot_general(
+                up_grad[...], w_buf[slot, 1, columns, :], across,
+                preferred_element_type=jnp.float32,
+            )
+            part = part.astype(prow.dtype)
+            for block in range(blocks):
+                prow[block, :main, columns] = part[block * main : (block + 1) * main]
+                prow[block, main:, columns] = part[blocks * main :]
+        d = shard(s)
+
+        def returned(block):
+            return jnp.dot(back[block], prow[block], preferred_element_type=jnp.float32)
+
+        for beside in range(PAIR):
+            away[d, beside] = returned(beside * PAIR + 1 - seat.core).astype(away.dtype)
+            to_twin(d, beside).start()
+        for beside in range(PAIR):
+            kept[d, beside] = returned(beside * PAIR + seat.core).astype(kept.dtype)
+
+    def products(k, _):
+        def one(j, carry):
+            product(PAIR * k + j)
+            return carry
+
+        lax.fori_loop(0, PAIR, one, 0)
+
+    def wide(ref):
+        return ref.astype(jnp.float32)
+
+    def pair_sum(k, _):
+        q = seat.line(k)
+        for b in (1, 0):
+            for a in (1, 0):
+                d, beside = seat.spot(q, a, b)
+                to_twin(d, beside).wait_recv()
+                total = wide(kept[d, beside]) + wide(came[d, beside])
+                n = q * PAIR + a
+                if b:
+                    out_last[n] = total.astype(out_last.dtype)
+                    to_last(n).start()
+                else:
+                    acc[n] = total
+
+    def last_sum(k, _):
+        q = seat.line(k)
+        for a in (1, 0):
+            n = q * PAIR + a
+            to_last(n).wait_recv()
+            total = acc[n] + wide(in_last[n])
+            if a:
+                out_first[q] = total.astype(out_first.dtype)
+                to_first(q).start()
+            else:
+                acc[n] = total
+
+    def first_sum(k, _):
+        q = seat.line(k)
+        n = q * PAIR
+        to_first(q).wait_recv()
+        acc[n] += wide(in_first[q])
+
+        @pl.when((q >= z) & seat.has_down)
+        def _():
+            to_up(q).wait_recv()
+            acc[n] += wide(in_up[q])
+
+        @pl.when((q <= z) & seat.has_up)
+        def _():
+            to_down(q).wait_recv()
+            acc[n] += wide(in_down[q])
+
+        @pl.when(q != z)
+        def _():
+            out_line[q] = acc[n].astype(out_line.dtype)
+
+        @pl.when(q > z)
+        def _():
+            to_up(q).start()
+
+        @pl.when(q < z)
+        def _():
+            to_down(q).start()
+
+        @pl.when(q == z)
+        def _():
+            out_ref[...] = acc[n].astype(out_ref.dtype)
+
+    run_plan(
+        depth,
+        (("mm", 0, 0), ("ps", 0, 0), ("ls", 0, BACK_LAGS[0]), ("fs", 0, BACK_LAGS[1])),
+        {"mm": products, "ps": pair_sum, "ls": last_sum, "fs": first_sum},
+    )
+
+    def settle(q, carry):
+        for j in range(PAIR):
+            to_last(q * PAIR + j).wait_send()
+            for beside in range(PAIR):
+                to_twin(q * PAIR + j, beside).wait_send()
+        to_first(q).wait_send()
+
+        @pl.when(q > z)
+        def _():
+            to_up(q).wait_send()
+
+        @pl.when(q < z)
+        def _():
+            to_down(q).wait_send()
+
+        return carry
+
+    lax.fori_loop(0, depth, settle, 0)
+
+
+def back_rows(depth, feat, gate_grad, up_grad, back, gate_w, up_w):
+    blocks, tok, slots = back.shape
+    count, hidden = gate_grad.shape
+    shards = depth * PAIR
+    vmem = pl.BlockSpec(memory_space=pltpu.VMEM)
+    anywhere = pl.BlockSpec(memory_space=pl.ANY)
+    half, wide = jnp.bfloat16, jnp.float32
+    dma = pltpu.SemaphoreType.DMA
+    piece = (tok, feat)
+    return pl.pallas_call(
+        functools.partial(back_kernel, depth, slots - ROW_TILE),
+        out_shape=jax.ShapeDtypeStruct(piece, half),
+        in_specs=[vmem, vmem, vmem, anywhere, anywhere],
+        out_specs=vmem,
+        scratch_shapes=[
+            pltpu.VMEM((blocks, slots, feat), half),
+            pltpu.VMEM((shards, PAIR) + piece, half),
+            pltpu.VMEM((shards, PAIR) + piece, half),
+            pltpu.VMEM((shards, PAIR) + piece, half),
+            pltpu.VMEM((shards,) + piece, wide),
+            pltpu.VMEM((shards,) + piece, half),
+            pltpu.VMEM((shards,) + piece, half),
+            pltpu.VMEM((depth,) + piece, half),
+            pltpu.VMEM((depth,) + piece, half),
+            pltpu.VMEM((depth,) + piece, half),
+            pltpu.VMEM((depth,) + piece, half),
+            pltpu.VMEM((depth,) + piece, half),
+            pltpu.VMEM((2, 2, feat, hidden), half),
+            dma((2, 2)),
+            dma((shards, PAIR)),
+            dma((shards, PAIR)),
+            dma((shards,)),
+            dma((shards,)),
+            dma((depth,)),
+            dma((depth,)),
+            dma((depth,)),
+            dma((2, depth)),
+        ],
+        compiler_params=pltpu.CompilerParams(
+            collective_id=3, has_side_effects=True, vmem_limit_bytes=VMEM_LIMIT
+        ),
+    )(gate_grad, up_grad, back, gate_w, up_w)
+
+
+def local_cube(
+    depth, tokens, cotangent, expert_ids, combine, w_gate, w_up, w_down, scale_vector
+):
+    feat = tokens.shape[1]
+    meta = jnp.concatenate(
+        [expert_ids.astype(jnp.float32).T, combine.T, jnp.zeros((4, tokens.shape[0]))], axis=0
+    )
+    gate_grad, up_grad, scale_grad, back = front(
+        depth, meta, tokens, cotangent, w_gate[0], w_up[0], w_down[0], scale_vector
+    )
+    token_grads = back_rows(depth, feat, gate_grad, up_grad, back, w_gate[0], w_up[0])
+    return token_grads, scale_grad
+
+
 def local(ring, tokens, cotangent, expert_ids, combine, w_gate, w_up, w_down, scale_vector):
     experts = lax.axis_size("expert")
     tok_count = tokens.shape[0]
@@ -392,8 +1020,13 @@
         P("expert", "dp", None),
         P("expert", "dp"),
     )
+    count = mesh.shape["dp"]
+    if mesh.shape["expert"] == PAIR * PAIR and count % PAIR == 0 and count <= SHORT_RING:
+        body = functools.partial(local_cube, count // PAIR)
+    else:
+        body = functools.partial(local, ring_order(mesh))
     return jax.shard_map(
-        functools.partial(local, ring_order(mesh)),
+        body,
         mesh=mesh,
         in_specs=placed,
         out_specs=(P("expert", "dp"), P("expert", "dp")),

time: 237 us -> 161 us (0.68)
  waiting for transfers between devices: 23.3 us -> 0 us
  matrix products: 20.2 us -> 0 us
  Pallas kernels: 171 us -> 156 us
  starting transfers between devices: 7.73 us -> 0 us
  local copies, waits for them, and re-layouts: 8.24 us -> 2.35 us
  other arithmetic: 5.62 us -> 2.03 us
    all_to_all x2 -> x0, waiting for transfers between devices: 23.3 us -> none  [the longest x1 15.1 us: local(): lax.all_to_all(sent, 'expert', split_axis=0, concat_axis=0, tiled=True)]
    dot_general x3 -> x0, matrix products: 20.2 us -> none  [the longest x1 18.6 us: local(): lax.dot_general(grads, down_w, (((1,), (1,)), ((), ())), preferred_elemen...]
    pallas_call x2, Pallas kernels: 171 us -> 156 us  [the longest x1 98.8 us: front(): pl.pallas_call(functools.partial(front_kernel, depth, main), out_shape=(j...]
    all_to_all x2 -> x0, starting transfers between devices: 7.73 us -> none  [the longest x1 4.26 us: local(): lax.all_to_all(sent, 'expert', split_axis=0, concat_axis=0, tiled=True)]
  transfers between devices with their start and end apart: 2 -> 0, of which waited for: 2 -> 0; matrix products, arithmetic and copies ran while one was open for 0% -> 0% of each run, Pallas kernels for 0% -> 0%
where the time goes in v1:
time: 161 us
  Pallas kernels  156 us (97%)
  local copies, waits for them, and re-layouts  2.35 us (1%)
  other arithmetic  2.03 us (1%)
    pallas_call x1, Pallas kernels, front(): pl.pallas_call(functools.partial(front_kernel, depth, main), out_shape=(j...  98.8 us
    pallas_call x1, Pallas kernels, back_rows(): pl.pallas_call(functools.partial(back_kernel, depth, slots - ROW_TILE), o...  56.7 us

profile of v1, /device:TPU:0, one launch (start us, length us, event | category | flops | bytes accessed | tf_op | source)
XLA Modules:
  0.0 160.6 jit_solution(14182149935648531522)
XLA Ops:
  0.6 0.1 pad.2.clone
  0.7 0.7 convert_bitcast_fusion
  1.4 1.3 maximum_maximum_fusion.meta_ref
  2.7 98.8 %shard_map.95 = (bf16[528,1792]{1,0:T(8,128)(2,1)}, bf16[528,1792]{1,0:T(8,128)(2,1)}, f32[1,1792]{1,0:T(1,128)}, bf16[4,256,144]{2,1,0:T(8,128)(2,1)}) custom-call(f32[8,256]{1,0:T(8,128)} %maximum_maximum_fusion.meta_ref, bf16[256,512]{1,0:T(8,128)(2,1)} %x_ref.1, bf16[256,512]{1,0:T(8,128)(2,1)} %g_ref.1, bf16[4096,1792]{1,0:T(8,128)(2,1)} %bitcast.6, ...), custom_call_target="tpu_custom_call" | custom-call | tf_op jit(solution)/shard_map/pallas_call | solution.py:691
  101.6 0.0 copy-start
  101.6 56.7 %shard_map.96 = bf16[256,512]{1,0:T(8,128)(2,1)} custom-call(bf16[528,1792]{1,0:T(8,128)(2,1)} %get-tuple-element.6.gate_grad, bf16[528,1792]{1,0:T(8,128)(2,1)} %get-tuple-element.7.up_grad, bf16[4,256,144]{2,1,0:T(8,128)(2,1)} %get-tuple-element.8.back, bf16[4096,1792]{1,0:T(8,128)(2,1)} %bitcast.7, bf16[4096,1792]{1,0:T(8,128)(2,1)} %bitcast.9), custom_call_target="tpu_custom_call" | custom-call | tf_op jit(solution)/shard_map/pallas_call | solution.py:918
  158.3 1.7 %copy.12 = bf16[256,512]{1,0:T(8,128)(2,1)} copy(bf16[256,512]{1,0:T(8,128)(2,1)} %shard_map.96) | data formatting | bytes 524288
  160.0 0.0 copy-done
  160.0 0.6 copy.13
  (1 shorter events, 0.0 us)
Async XLA Ops:
  101.6 58.4 %copy-start = (f32[1,1792]{1,0:T(1,128)S(1)}, f32[1,1792]{1,0:T(1,128)}, u32[]{:S(2)}) copy-start(f32[1,1792]{1,0:T(1,128)} %get-tuple-element.13) | copy-start | bytes 21508

commit v2 on v1

--- a/solution.py
+++ b/solution.py
@@ -339,11 +339,30 @@
 PAIR = 2
 TILE = 256
 UP, DOWN, FIRST, LAST, TWIN = range(5)
+LATE, EARLY = 0, 1
 FRONT_PLAN = (
-    ("xl", 0, 0), ("xa", 0, 0), ("xb", 0, 1), ("gl", 0, 1), ("gl", 1, 1), ("xb", 1, 1),
-    ("gb", 0, 2), ("gb", 1, 2), ("cx", 0, 2), ("cx", 1, 2), ("cg", 0, 3), ("cg", 1, 3),
+    ("xl", 0, 2),
+    ("xb", 1, 4),
+    ("cg", 0, 2),
+    ("gb", 1, 2),
+    ("gl", 1, 1),
+    ("cx", 1, 5),
+    ("gl", 0, 0),
+    ("xb", 0, 3),
+    ("cg", 1, 2),
+    ("xa", 0, 2),
+    ("cx", 0, 3),
+    ("gb", 0, 1),
 )
-BACK_LAGS = (2, 3)
+BACK_PLAN = (
+    ("ps", 0, 1),
+    ("fs", 0, 4),
+    ("mm", 0, 0),
+    ("ps", 1, 2),
+    ("mm", 1, 1),
+    ("ls", 0, 3),
+    ("ls", 1, 2),
+)
 
 
 def near_first(depth):
@@ -355,14 +374,13 @@
 
 
 class Seat:
-    def __init__(self, depth, far):
+    def __init__(self, depth):
         self.depth = depth
         self.dp = lax.axis_index("dp")
         self.expert = lax.axis_index("expert")
         self.z, self.x = lax.div(self.dp, PAIR), lax.rem(self.dp, PAIR)
         self.y, self.core = lax.div(self.expert, PAIR), lax.rem(self.expert, PAIR)
-        table = near_first(depth)
-        self.table = [q for row in table for q in (row[::-1] if far else row)]
+        self.table = [q for row in near_first(depth) for q in row]
         core, dp, expert = self.core, self.dp, self.expert
         dx, dy = 1 - 2 * self.x, 2 - 4 * self.y
         self.twin = {"dp": dp, "expert": expert + 1 - 2 * core}
@@ -379,6 +397,9 @@
     def line(self, k):
         return lookup(self.table, self.z * self.depth + k)
 
+    def far(self, k):
+        return self.line(self.depth - 1 - k)
+
     def spot(self, q, a, b):
         core = self.core
         across = lax.rem(self.x + a + core * (b - a), PAIR)
@@ -428,29 +449,41 @@
     lax.fori_loop(0, span, turn, 0)
 
 
-def front_kernel(
-    depth, main, meta_ref, x_ref, g_ref, gate_w, up_w, down_w, scale_ref, gate_ref, up_ref,
-    total_ref, back_ref, full, meta, hot, weight, rows, gate, up, hid, w_buf, d_buf, total,
-    own_sem, w_sem, d_sem, note_send, note_recv, send_sem, recv_sem,
+def cube_kernel(
+    depth, main, ids_ref, share_ref, x_ref, g_ref, gate_w, up_w, down_w, scale_ref, out_ref, total_ref,
+    full, ids, shares, hot, back, weight, rows, gate, up, hid, w_buf, d_buf, total, gate_grad, up_grad,
+    prow, came, acc, in_last, in_first, in_up, in_down, own_sem, w_sem, d_sem, note_send,
+    note_recv, send_sem, recv_sem, twin_send, twin_recv, last_send, last_recv, first_send,
+    first_recv, line_send, line_recv,
 ):
-    seat = Seat(depth, False)
+    seat = Seat(depth)
     blocks = PAIR * PAIR
     feat = x_ref.shape[1]
     tok = x_ref.shape[0]
     hidden = gate.shape[1]
     slots = hot.shape[1]
     tile = TILE if hidden % TILE == 0 else hidden
+    back_tile = TILE if feat % TILE == 0 else feat
     z = seat.z
 
     def shard(k, a):
         return seat.line(k) * PAIR + lax.rem(seat.x + a, PAIR)
 
+    def load_lines(d, slot):
+        lines = pl.ds(pl.multiple_of(d * feat, feat), feat)
+        return (
+            pltpu.make_async_copy(gate_w.at[lines, :], w_buf.at[slot, 0], w_sem.at[slot, 0]),
+            pltpu.make_async_copy(up_w.at[lines, :], w_buf.at[slot, 1], w_sem.at[slot, 1]),
+        )
+
     def load_up(k, a):
-        lines = pl.ds(pl.multiple_of(shard(k, a) * feat, feat), feat)
-        return (
-            pltpu.make_async_copy(gate_w.at[lines, :], w_buf.at[a, 0], w_sem.at[a, 0]),
-            pltpu.make_async_copy(up_w.at[lines, :], w_buf.at[a, 1], w_sem.at[a, 1]),
-        )
+        return load_lines(shard(k, a), a)
+
+    def back_shard(k, j):
+        return seat.far(k) * PAIR + lax.rem(seat.x + 1 + j, PAIR)
+
+    def load_back(k, j):
+        return load_lines(back_shard(k, j), j)
 
     def load_down(k, a):
         columns = pl.ds(pl.multiple_of(shard(k, a) * feat, feat), feat)
@@ -462,16 +495,21 @@
     ]
     for copy in own:
         copy.start()
-    meta[seat.expert] = meta_ref[...]
+    ids[seat.expert] = ids_ref[...]
+    shares[seat.expert] = share_ref[...]
     seat.greet()
 
-    def note(n, target):
+    def note(n, ref, table, place, target):
         return remote(
-            meta_ref, meta.at[seat.expert], note_send.at[n], note_recv.at[seat.expert], target
-        )
-
+            ref, table.at[seat.expert], note_send.at[n, place], note_recv.at[n, seat.expert], target
+        )
+
+    peers = (seat.twin, seat.across_y, seat.corner)
+    tables = ((ids_ref, ids), (share_ref, shares))
     notes = [
-        note(n, target) for n, target in enumerate((seat.twin, seat.across_y, seat.corner))
+        note(n, ref, table, place, target)
+        for place, target in enumerate(peers)
+        for n, (ref, table) in enumerate(tables)
     ]
 
     def link(t, q, a, b, kind):
@@ -502,21 +540,18 @@
     def drain(copy):
         copy.wait_send()
 
-    def x_line(k, _):
+    def early_line(k, _):
         q = seat.line(k)
-
-        @pl.when(k > 0)
-        def _():
-            arrived(0, q, 0, 0)
-            along(0, q, 0, begin)
-            for kind in (FIRST, LAST, TWIN):
-                link(0, q, 0, 0, kind).start()
-
-    def x_first(k, _):
+        pl.when(k > 0)(lambda: arrived(EARLY, q, 0, 0))
+        along(EARLY, q, 0, begin)
+        for kind in (FIRST, LAST, TWIN):
+            link(EARLY, q, 0, 0, kind).start()
+
+    def early_first(k, _):
         q = seat.line(k)
-        arrived(0, q, 1, 0)
-        link(0, q, 1, 0, LAST).start()
-        link(0, q, 1, 0, TWIN).start()
+        arrived(EARLY, q, 1, 0)
+        link(EARLY, q, 1, 0, LAST).start()
+        link(EARLY, q, 1, 0, TWIN).start()
 
     def from_last(t):
         def op(k, a):
@@ -526,14 +561,14 @@
 
         return op
 
-    def g_line(k, a):
+    def late_line(k, a):
         q = seat.line(k)
 
         def pass_on():
-            arrived(1, q, a, 0)
-            along(1, q, a, begin)
-            link(1, q, a, 0, LAST).start()
-            link(1, q, a, 0, TWIN).start()
+            arrived(LATE, q, a, 0)
+            along(LATE, q, a, begin)
+            link(LATE, q, a, 0, LAST).start()
+            link(LATE, q, a, 0, TWIN).start()
 
         if a:
             pass_on()
@@ -574,6 +609,11 @@
                 )
         again(load_up, k, a)
 
+        @pl.when(k + 1 == depth)
+        def _():
+            for copy in load_back(0, a):
+                copy.start()
+
     def g_products(k, a):
         dispatch(1, shard(k, a))
         for copy in load_down(k, a):
@@ -590,12 +630,9 @@
         copy.wait()
     for copy in notes:
         copy.start()
-    along(0, z, 0, begin)
     for kind in (FIRST, LAST, TWIN):
-        link(0, z, 0, 0, kind).start()
-    along(1, z, 0, begin)
-    for kind in (FIRST, LAST, TWIN):
-        link(1, z, 0, 0, kind).start()
+        link(LATE, z, 0, 0, kind).start()
+    along(LATE, z, 0, begin)
     for a in range(PAIR):
         for copy in load_up(0, a) + load_down(0, a):
             copy.start()
@@ -607,16 +644,19 @@
     before = (down_rows < over_columns).astype(jnp.bfloat16)
     slot_rows = lax.broadcasted_iota(jnp.int32, (slots, tok), 0).astype(jnp.float32)
     slot_columns = lax.broadcasted_iota(jnp.int32, (tok, slots), 1).astype(jnp.float32)
-    mine = seat.expert.astype(jnp.float32)
-    for n, target in enumerate((seat.twin, seat.across_y, seat.corner)):
+    same = down_rows == over_columns
+    for target in peers:
         other = target["expert"]
-        remote(
-            meta_ref, meta.at[other], note_send.at[n], note_recv.at[other], target
-        ).wait_recv()
+        for n, (ref, table) in enumerate(tables):
+            remote(
+                ref, table.at[other], note_send.at[n, 0], note_recv.at[n, other], target
+            ).wait_recv()
     for block in range(blocks):
-        notes_in = meta[block]
-        named = (notes_in[0:PAIR] == mine).astype(jnp.float32)
-        hit = named[0:1] + named[1:PAIR]
+        named = (ids[block] == seat.expert).astype(jnp.float32)
+        hit_column = jnp.sum(named, axis=1, keepdims=True)
+        share_column = jnp.sum(named * shares[block], axis=1, keepdims=True)
+        hit = jnp.sum(jnp.where(same, hit_column, 0.0), axis=0, keepdims=True)
+        share = jnp.sum(jnp.where(same, share_column, 0.0), axis=0, keepdims=True)
         earlier = jnp.dot(
             jnp.broadcast_to(hit, (8, tok)).astype(jnp.bfloat16), before,
             preferred_element_type=jnp.float32,
@@ -625,18 +665,17 @@
         want = jnp.where(hit > 0, spilled, -1.0)
         chosen = (slot_rows == want).astype(jnp.float32)
         hot[block] = chosen.astype(hot.dtype)
-        share = named[0:1] * notes_in[PAIR : PAIR + 1] + named[1:2] * notes_in[PAIR + 1 : PAIR + 2]
         weight[block] = jnp.sum(chosen * share, axis=1, keepdims=True)
         want_column = jnp.sum(
-            jnp.where(down_rows == over_columns, want, 0.0), axis=1, keepdims=True
-        )
-        back_ref[block] = (slot_columns == want_column).astype(back_ref.dtype)
+            jnp.where(same, want, 0.0), axis=1, keepdims=True
+        )
+        back[block] = (slot_columns == want_column).astype(back.dtype)
 
     run_plan(
         depth, FRONT_PLAN,
         {
-            "xl": x_line, "xa": x_first, "xb": from_last(0), "gl": g_line, "gb": from_last(1),
-            "cx": x_products, "cg": g_products,
+            "xl": early_line, "xa": early_first, "xb": from_last(EARLY), "gl": late_line,
+            "gb": from_last(LATE), "cx": g_products, "cg": x_products,
         },
     )
 
@@ -649,10 +688,10 @@
         silu_gate = gate_act * sigmoid_gate
         total[...] += hidden_grad * silu_gate * up_act
         scaled_grad = hidden_grad * scale_ref[...]
-        up_ref[lines, :] = (scaled_grad * silu_gate).astype(up_ref.dtype)
-        gate_ref[lines, :] = (
+        up_grad[lines, :] = (scaled_grad * silu_gate).astype(up_grad.dtype)
+        gate_grad[lines, :] = (
             scaled_grad * up_act * sigmoid_gate * (1.0 + gate_act * (1.0 - sigmoid_gate))
-        ).astype(gate_ref.dtype)
+        ).astype(gate_grad.dtype)
         return carry
 
     lax.fori_loop(0, gate.shape[0] // step, finish, 0)
@@ -664,19 +703,184 @@
     def settle(k, carry):
         for t in range(2):
             for a in range(PAIR):
-                if t or not a:
+                if t == LATE or not a:
                     along(t, k, a, drain)
                 for b in range(PAIR):
                     link(t, k, a, b, TWIN).wait_send()
                 link(t, k, a, 0, LAST).wait_send()
-        link(0, k, 0, 0, FIRST).wait_send()
+        link(EARLY, k, 0, 0, FIRST).wait_send()
         return carry
 
     lax.fori_loop(0, depth, settle, 0)
-    link(1, z, 0, 0, FIRST).wait_send()
-
-
-def front(depth, meta, tokens, cotangent, gate_w, up_w, down_w, scale):
+    link(LATE, z, 0, 0, FIRST).wait_send()
+
+    def kept(d, beside):
+        return full.at[0, d, beside]
+
+    def away(d, beside):
+        return full.at[0, d, PAIR + beside]
+
+    def out_last(n):
+        return full.at[1, n, 0]
+
+    def out_first(q):
+        return full.at[1, q, 1]
+
+    def out_line(q):
+        return full.at[1, q, 2]
+
+    def to_twin(d, beside):
+        return remote(
+            away(d, beside), came.at[d, beside], twin_send.at[d, beside],
+            twin_recv.at[d, beside], seat.twin,
+        )
+
+    def to_last(n):
+        return remote(
+            out_last(n), in_last.at[n], last_send.at[n], last_recv.at[n], seat.last
+        )
+
+    def to_first(q):
+        return remote(
+            out_first(q), in_first.at[q], first_send.at[q], first_recv.at[q], seat.first
+        )
+
+    def to_up(q):
+        return remote(
+            out_line(q), in_up.at[q], line_send.at[q], line_recv.at[0, q], seat.up
+        )
+
+    def to_down(q):
+        return remote(
+            out_line(q), in_down.at[q], line_send.at[q], line_recv.at[1, q], seat.down
+        )
+
+    def product(k, j):
+        for copy in load_back(k, j):
+            copy.wait()
+        across = (((1,), (1,)), ((), ()))
+        for n in range(0, feat, back_tile):
+            columns = slice(n, n + back_tile)
+            part = lax.dot_general(
+                gate_grad[...], w_buf[j, 0, columns, :], across,
+                preferred_element_type=jnp.float32,
+            ) + lax.dot_general(
+                up_grad[...], w_buf[j, 1, columns, :], across,
+                preferred_element_type=jnp.float32,
+            )
+            part = part.astype(prow.dtype)
+            for block in range(blocks):
+                prow[block, :main, columns] = part[block * main : (block + 1) * main]
+                prow[block, main:, columns] = part[blocks * main :]
+
+        @pl.when(k + 1 < depth)
+        def _():
+            for copy in load_back(k + 1, j):
+                copy.start()
+
+        d = back_shard(k, j)
+
+        def returned(block):
+            return jnp.dot(back[block], prow[block], preferred_element_type=jnp.float32)
+
+        for beside in range(PAIR):
+            away(d, beside)[...] = returned(beside * PAIR + 1 - seat.core).astype(full.dtype)
+            to_twin(d, beside).start()
+        for beside in range(PAIR):
+            kept(d, beside)[...] = returned(beside * PAIR + seat.core).astype(full.dtype)
+
+    def wide(ref):
+        return ref.astype(jnp.float32)
+
+    def pair_sum(k, j):
+        q = seat.far(k)
+        core = seat.core
+        for n in (1, 0):
+            a = core * n + (1 - core) * (1 - j)
+            b = core * (1 - j) + (1 - core) * n
+            d, beside = seat.spot(q, a, b)
+            to_twin(d, beside).wait_recv()
+            total = wide(kept(d, beside)[...]) + wide(came[d, beside])
+            m = q * PAIR + a
+
+            @pl.when(b == 1)
+            def _(m=m, total=total):
+                out_last(m)[...] = total.astype(full.dtype)
+                to_last(m).start()
+
+            @pl.when(b == 0)
+            def _(m=m, total=total):
+                acc[m] = total
+
+    def last_sum(k, a):
+        q = seat.far(k)
+        n = q * PAIR + a
+        to_last(n).wait_recv()
+        if a:
+            out_first(q)[...] = (acc[n] + wide(in_last[n])).astype(full.dtype)
+            to_first(q).start()
+        else:
+            acc[n] += wide(in_last[n])
+
+    def first_sum(k, _):
+        q = seat.far(k)
+        n = q * PAIR
+        to_first(q).wait_recv()
+        acc[n] += wide(in_first[q])
+
+        @pl.when((q >= z) & seat.has_down)
+        def _():
+            to_up(q).wait_recv()
+            acc[n] += wide(in_up[q])
+
+        @pl.when((q <= z) & seat.has_up)
+        def _():
+            to_down(q).wait_recv()
+            acc[n] += wide(in_down[q])
+
+        @pl.when(q != z)
+        def _():
+            out_line(q)[...] = acc[n].astype(full.dtype)
+
+        @pl.when(q > z)
+        def _():
+            to_up(q).start()
+
+        @pl.when(q < z)
+        def _():
+            to_down(q).start()
+
+        @pl.when(q == z)
+        def _():
+            out_ref[...] = acc[n].astype(out_ref.dtype)
+
+    run_plan(
+        depth,
+        BACK_PLAN,
+        {"mm": product, "ps": pair_sum, "ls": last_sum, "fs": first_sum},
+    )
+
+    def settle_back(q, carry):
+        for j in range(PAIR):
+            to_last(q * PAIR + j).wait_send()
+            for beside in range(PAIR):
+                to_twin(q * PAIR + j, beside).wait_send()
+        to_first(q).wait_send()
+
+        @pl.when(q > z)
+        def _():
+            to_up(q).wait_send()
+
+        @pl.when(q < z)
+        def _():
+            to_down(q).wait_send()
+
+        return carry
+
+    lax.fori_loop(0, depth, settle_back, 0)
+
+
+def cube(depth, expert_ids, combine, tokens, cotangent, gate_w, up_w, down_w, scale):
     tok, feat = tokens.shape
     hidden = gate_w.shape[1]
     blocks = PAIR * PAIR
@@ -688,20 +892,21 @@
     anywhere = pl.BlockSpec(memory_space=pl.ANY)
     half, wide = jnp.bfloat16, jnp.float32
     dma = pltpu.SemaphoreType.DMA
+    piece = (tok, feat)
     return pl.pallas_call(
-        functools.partial(front_kernel, depth, main),
+        functools.partial(cube_kernel, depth, main),
         out_shape=(
-            jax.ShapeDtypeStruct((count, hidden), half),
-            jax.ShapeDtypeStruct((count, hidden), half),
+            jax.ShapeDtypeStruct(piece, half),
             jax.ShapeDtypeStruct((1, hidden), wide),
-            jax.ShapeDtypeStruct((blocks, tok, slots), half),
         ),
-        in_specs=[vmem] + [anywhere] * 5 + [vmem],
-        out_specs=(vmem, vmem, vmem, vmem),
+        in_specs=[vmem, vmem] + [anywhere] * 5 + [vmem],
+        out_specs=(vmem, vmem),
         scratch_shapes=[
-            pltpu.VMEM((2, shards, blocks, tok, feat), half),
-            pltpu.VMEM((blocks,) + meta.shape, wide),
+            pltpu.VMEM((2, shards, blocks) + piece, half),
+            pltpu.VMEM((blocks,) + expert_ids.shape, jnp.int32),
+            pltpu.VMEM((blocks,) + combine.shape, wide),
             pltpu.VMEM((blocks, slots, tok), half),
+            pltpu.VMEM((blocks, tok, slots), half),
             pltpu.VMEM((blocks, slots, 1), wide),
             pltpu.VMEM((count, feat), half),
             pltpu.VMEM((count, hidden), wide),
@@ -710,231 +915,22 @@
             pltpu.VMEM((PAIR, 2, feat, hidden), half),
             pltpu.VMEM((PAIR, hidden, feat), half),
             pltpu.VMEM((ROW_TILE, hidden), wide),
-            dma((2,)),
-            dma((PAIR, 2)),
-            dma((PAIR,)),
-            dma((3,)),
-            dma((blocks,)),
-            dma((2, 5, depth * blocks)),
-            dma((2, shards, blocks)),
-        ],
-        compiler_params=pltpu.CompilerParams(
-            collective_id=2, has_side_effects=True, vmem_limit_bytes=VMEM_LIMIT
-        ),
-    )(meta, tokens, cotangent, gate_w, up_w, down_w, scale)
-
-
-def back_kernel(
-    depth, main, gate_grad, up_grad, back, gate_w, up_w, out_ref, prow, kept, away, came, acc,
-    out_last, in_last, out_first, in_first, out_line, in_up, in_down, w_buf, w_sem, twin_send,
-    twin_recv, last_send, last_recv, first_send, first_recv, line_send, line_recv,
-):
-    seat = Seat(depth, True)
-    blocks = PAIR * PAIR
-    tok, feat = out_ref.shape
-    shards = depth * PAIR
-    tile = TILE if feat % TILE == 0 else feat
-    z = seat.z
-
-    def shard(s):
-        return seat.line(lax.div(s, PAIR)) * PAIR + lax.rem(seat.x + 1 + s, PAIR)
-
-    def load(s):
-        slot = lax.rem(s, 2)
-        lines = pl.ds(pl.multiple_of(shard(s) * feat, feat), feat)
-        return (
-            pltpu.make_async_copy(gate_w.at[lines, :], w_buf.at[slot, 0], w_sem.at[slot, 0]),
-            pltpu.make_async_copy(up_w.at[lines, :], w_buf.at[slot, 1], w_sem.at[slot, 1]),
-        )
-
-    for copy in load(0):
-        copy.start()
-    seat.greet()
-
-    def to_twin(d, beside):
-        return remote(
-            away.at[d, beside], came.at[d, beside], twin_send.at[d, beside],
-            twin_recv.at[d, beside], seat.twin,
-        )
-
-    def to_last(n):
-        return remote(
-            out_last.at[n], in_last.at[n], last_send.at[n], last_recv.at[n], seat.last
-        )
-
-    def to_first(q):
-        return remote(
-            out_first.at[q], in_first.at[q], first_send.at[q], first_recv.at[q], seat.first
-        )
-
-    def to_up(q):
-        return remote(
-            out_line.at[q], in_up.at[q], line_send.at[q], line_recv.at[0, q], seat.up
-        )
-
-    def to_down(q):
-        return remote(
-            out_line.at[q], in_down.at[q], line_send.at[q], line_recv.at[1, q], seat.down
-        )
-
-    def product(s):
-        slot = lax.rem(s, 2)
-
-        @pl.when(s + 1 < shards)
-        def _():
-            for copy in load(s + 1):
-                copy.start()
-
-        for copy in load(s):
-            copy.wait()
-        across = (((1,), (1,)), ((), ()))
-        for n in range(0, feat, tile):
-            columns = slice(n, n + tile)
-            part = lax.dot_general(
-                gate_grad[...], w_buf[slot, 0, columns, :], across,
-                preferred_element_type=jnp.float32,
-            ) + lax.dot_general(
-                up_grad[...], w_buf[slot, 1, columns, :], across,
-                preferred_element_type=jnp.float32,
-            )
-            part = part.astype(prow.dtype)
-            for block in range(blocks):
-                prow[block, :main, columns] = part[block * main : (block + 1) * main]
-                prow[block, main:, columns] = part[blocks * main :]
-        d = shard(s)
-
-        def returned(block):
-            return jnp.dot(back[block], prow[block], preferred_element_type=jnp.float32)
-
-        for beside in range(PAIR):
-            away[d, beside] = returned(beside * PAIR + 1 - seat.core).astype(away.dtype)
-            to_twin(d, beside).start()
-        for beside in range(PAIR):
-            kept[d, beside] = returned(beside * PAIR + seat.core).astype(kept.dtype)
-
-    def products(k, _):
-        def one(j, carry):
-            product(PAIR * k + j)
-            return carry
-
-        lax.fori_loop(0, PAIR, one, 0)
-
-    def wide(ref):
-        return ref.astype(jnp.float32)
-
-    def pair_sum(k, _):
-        q = seat.line(k)
-        for b in (1, 0):
-            for a in (1, 0):
-                d, beside = seat.spot(q, a, b)
-                to_twin(d, beside).wait_recv()
-                total = wide(kept[d, beside]) + wide(came[d, beside])
-                n = q * PAIR + a
-                if b:
-                    out_last[n] = total.astype(out_last.dtype)
-                    to_last(n).start()
-                else:
-                    acc[n] = total
-
-    def last_sum(k, _):
-        q = seat.line(k)
-        for a in (1, 0):
-            n = q * PAIR + a
-            to_last(n).wait_recv()
-            total = acc[n] + wide(in_last[n])
-            if a:
-                out_first[q] = total.astype(out_first.dtype)
-                to_first(q).start()
-            else:
-                acc[n] = total
-
-    def first_sum(k, _):
-        q = seat.line(k)
-        n = q * PAIR
-        to_first(q).wait_recv()
-        acc[n] += wide(in_first[q])
-
-        @pl.when((q >= z) & seat.has_down)
-        def _():
-            to_up(q).wait_recv()
-            acc[n] += wide(in_up[q])
-
-        @pl.when((q <= z) & seat.has_up)
-        def _():
-            to_down(q).wait_recv()
-            acc[n] += wide(in_down[q])
-
-        @pl.when(q != z)
-        def _():
-            out_line[q] = acc[n].astype(out_line.dtype)
-
-        @pl.when(q > z)
-        def _():
-            to_up(q).start()
-
-        @pl.when(q < z)
-        def _():
-            to_down(q).start()
-
-        @pl.when(q == z)
-        def _():
-            out_ref[...] = acc[n].astype(out_ref.dtype)
-
-    run_plan(
-        depth,
-        (("mm", 0, 0), ("ps", 0, 0), ("ls", 0, BACK_LAGS[0]), ("fs", 0, BACK_LAGS[1])),
-        {"mm": products, "ps": pair_sum, "ls": last_sum, "fs": first_sum},
-    )
-
-    def settle(q, carry):
-        for j in range(PAIR):
-            to_last(q * PAIR + j).wait_send()
-            for beside in range(PAIR):
-                to_twin(q * PAIR + j, beside).wait_send()
-        to_first(q).wait_send()
-
-        @pl.when(q > z)
-        def _():
-            to_up(q).wait_send()
-
-        @pl.when(q < z)
-        def _():
-            to_down(q).wait_send()
-
-        return carry
-
-    lax.fori_loop(0, depth, settle, 0)
-
-
-def back_rows(depth, feat, gate_grad, up_grad, back, gate_w, up_w):
-    blocks, tok, slots = back.shape
-    count, hidden = gate_grad.shape
-    shards = depth * PAIR
-    vmem = pl.BlockSpec(memory_space=pltpu.VMEM)
-    anywhere = pl.BlockSpec(memory_space=pl.ANY)
-    half, wide = jnp.bfloat16, jnp.float32
-    dma = pltpu.SemaphoreType.DMA
-    piece = (tok, feat)
-    return pl.pallas_call(
-        functools.partial(back_kernel, depth, slots - ROW_TILE),
-        out_shape=jax.ShapeDtypeStruct(piece, half),
-        in_specs=[vmem, vmem, vmem, anywhere, anywhere],
-        out_specs=vmem,
-        scratch_shapes=[
+            pltpu.VMEM((count, hidden), half),
+            pltpu.VMEM((count, hidden), half),
             pltpu.VMEM((blocks, slots, feat), half),
             pltpu.VMEM((shards, PAIR) + piece, half),
-            pltpu.VMEM((shards, PAIR) + piece, half),
-            pltpu.VMEM((shards, PAIR) + piece, half),
             pltpu.VMEM((shards,) + piece, wide),
-            pltpu.VMEM((shards,) + piece, half),
             pltpu.VMEM((shards,) + piece, half),
             pltpu.VMEM((depth,) + piece, half),
             pltpu.VMEM((depth,) + piece, half),
             pltpu.VMEM((depth,) + piece, half),
-            pltpu.VMEM((depth,) + piece, half),
-            pltpu.VMEM((depth,) + piece, half),
-            pltpu.VMEM((2, 2, feat, hidden), half),
-            dma((2, 2)),
+            dma((2,)),
+            dma((PAIR, 2)),
+            dma((PAIR,)),
+            dma((2, 3)),
+            dma((2, blocks)),
+            dma((2, 5, depth * blocks)),
+            dma((2, shards, blocks)),
             dma((shards, PAIR)),
             dma((shards, PAIR)),
             dma((shards,)),
@@ -945,23 +941,17 @@
             dma((2, depth)),
         ],
         compiler_params=pltpu.CompilerParams(
-            collective_id=3, has_side_effects=True, vmem_limit_bytes=VMEM_LIMIT
+            collective_id=2, has_side_effects=True, vmem_limit_bytes=VMEM_LIMIT
         ),
-    )(gate_grad, up_grad, back, gate_w, up_w)
+    )(expert_ids, combine, tokens, cotangent, gate_w, up_w, down_w, scale)
 
 
 def local_cube(
     depth, tokens, cotangent, expert_ids, combine, w_gate, w_up, w_down, scale_vector
 ):
-    feat = tokens.shape[1]
-    meta = jnp.concatenate(
-        [expert_ids.astype(jnp.float32).T, combine.T, jnp.zeros((4, tokens.shape[0]))], axis=0
+    return cube(
+        depth, expert_ids, combine, tokens, cotangent, w_gate[0], w_up[0], w_down[0], scale_vector
     )
-    gate_grad, up_grad, scale_grad, back = front(
-        depth, meta, tokens, cotangent, w_gate[0], w_up[0], w_down[0], scale_vector
-    )
-    token_grads = back_rows(depth, feat, gate_grad, up_grad, back, w_gate[0], w_up[0])
-    return token_grads, scale_grad
 
 
 def local(ring, tokens, cotangent, expert_ids, combine, w_gate, w_up, w_down, scale_vector):

time: 161 us -> 149 us (0.925)
  Pallas kernels: 156 us -> 142 us
  local copies, waits for them, and re-layouts: 2.35 us -> 5.91 us
  other arithmetic: 2.03 us -> 0 us
    pallas_call x2 -> x1, Pallas kernels: 156 us -> 142 us  [cube(): pl.pallas_call(functools.partial(cube_kernel, depth, main), out_shape=(ja...]
    unnamed x4, local copies, waits for them, and re-layouts: 2.27 us -> 5.91 us
where the time goes in v2:
time: 149 us
  Pallas kernels  142 us (95%)
  local copies, waits for them, and re-layouts  5.91 us (4%)
    pallas_call x1, Pallas kernels, cube(): pl.pallas_call(functools.partial(cube_kernel, depth, main), out_shape=(ja...  142 us
    unnamed x4, local copies, waits for them, and re-layouts  5.91 us

profile of v2, /device:TPU:0, one launch (start us, length us, event | category | flops | bytes accessed | tf_op | source)
XLA Modules:
  0.0 148.9 jit_solution(9280127714619545528)
XLA Ops:
  0.6 1.5 copy.10.ids_ref
  2.1 1.5 copy.11.share_ref
  3.6 142.4 %shard_map.95 = (bf16[256,512]{1,0:T(8,128)(2,1)}, f32[1,1792]{1,0:T(1,128)}) custom-call(s32[256,2]{1,0:T(8,128)} %copy.10.ids_ref, f32[256,2]{1,0:T(8,128)} %copy.11.share_ref, bf16[256,512]{1,0:T(8,128)(2,1)} %x_ref.1, bf16[256,512]{1,0:T(8,128)(2,1)} %g_ref.1, bf16[4096,1792]{1,0:T(8,128)(2,1)} %bitcast.3, bf16[4096,1792]{1,0:T(8,128)(2,1)} %bitcast.4, ...), custom_call_target="tpu_custom_call" | custom-call | tf_op jit(solution)/shard_map/pallas_call | solution.py:896
  146.0 1.7 %copy.14 = bf16[256,512]{1,0:T(8,128)(2,1)} copy(bf16[256,512]{1,0:T(8,128)(2,1)} %get-tuple-element.4) | data formatting | bytes 524288
  147.7 1.3 copy.15

commit v3 on v2

--- a/solution.py
+++ b/solution.py
@@ -339,29 +339,26 @@
 PAIR = 2
 TILE = 256
 UP, DOWN, FIRST, LAST, TWIN = range(5)
-LATE, EARLY = 0, 1
+LATE, EARLY = 1, 0
 FRONT_PLAN = (
-    ("xl", 0, 2),
-    ("xb", 1, 4),
-    ("cg", 0, 2),
-    ("gb", 1, 2),
-    ("gl", 1, 1),
-    ("cx", 1, 5),
-    ("gl", 0, 0),
-    ("xb", 0, 3),
-    ("cg", 1, 2),
-    ("xa", 0, 2),
-    ("cx", 0, 3),
-    ("gb", 0, 1),
+    ("xl", 0, 0), ("gl", 0, 0), ("xl", 1, 0), ("xa", 0, 0), ("xb", 0, 0),
+    ("xl", 2, 0), ("gl", 0, 1), ("xb", 1, 0), ("xa", 1, 0), ("cx", 0, 0),
+    ("xl", 3, 0), ("gl", 1, 0), ("cx", 1, 0), ("xb", 0, 1), ("gl", 1, 1),
+    ("xa", 2, 0), ("cx", 0, 1), ("gl", 2, 0), ("xb", 2, 0), ("gb", 0, 0),
+    ("cx", 2, 0), ("xa", 3, 0), ("cg", 0, 0), ("gb", 0, 1), ("gl", 2, 1),
+    ("xb", 1, 1), ("cg", 0, 1), ("cx", 1, 1), ("gl", 3, 0), ("gb", 1, 0),
+    ("xb", 3, 0), ("cg", 1, 0), ("cx", 3, 0), ("gb", 1, 1), ("gl", 3, 1),
+    ("xb", 3, 1), ("xb", 2, 1), ("cg", 1, 1), ("cx", 2, 1), ("gb", 3, 0),
+    ("gb", 2, 1), ("gb", 2, 0), ("cg", 2, 0), ("cg", 3, 0), ("gb", 3, 1),
+    ("cx", 3, 1), ("cg", 2, 1), ("cg", 3, 1),
 )
 BACK_PLAN = (
-    ("ps", 0, 1),
-    ("fs", 0, 4),
-    ("mm", 0, 0),
-    ("ps", 1, 2),
-    ("mm", 1, 1),
-    ("ls", 0, 3),
-    ("ls", 1, 2),
+    ("mm", 0, 0), ("mm", 0, 1), ("ps", 0, 0), ("mm", 1, 0), ("ps", 0, 1),
+    ("mm", 2, 0), ("ls", 0, 1), ("ps", 1, 0), ("mm", 1, 1), ("mm", 2, 1),
+    ("ps", 2, 0), ("ps", 1, 1), ("ls", 0, 0), ("ps", 2, 1), ("fs", 0, 0),
+    ("ls", 1, 1), ("mm", 3, 0), ("ls", 2, 1), ("mm", 3, 1), ("ps", 3, 0),
+    ("ps", 3, 1), ("ls", 1, 0), ("fs", 1, 0), ("ls", 2, 0), ("fs", 2, 0),
+    ("ls", 3, 1), ("ls", 3, 0), ("fs", 3, 0),
 )
 
 
@@ -435,23 +432,26 @@
 
 
 def run_plan(depth, plan, ops):
-    span = depth + max(lag for _, _, lag in plan)
+    names = sorted({(name, part) for name, _, part in plan})
+    codes = [names.index((name, part)) * depth + k for name, k, part in plan]
 
     def turn(i, carry):
-        for name, part, lag in plan:
-
-            @pl.when((i >= lag) & (i < lag + depth))
-            def _(name=name, part=part, lag=lag):
-                ops[name](i - lag, part)
+        code = lookup(codes, i)
+        which, k = lax.div(code, depth), lax.rem(code, depth)
+        for index, (name, part) in enumerate(names):
+
+            @pl.when(which == index)
+            def _(name=name, part=part):
+                ops[name](k, part)
 
         return carry
 
-    lax.fori_loop(0, span, turn, 0)
+    lax.fori_loop(0, len(codes), turn, 0)
 
 
 def cube_kernel(
     depth, main, ids_ref, share_ref, x_ref, g_ref, gate_w, up_w, down_w, scale_ref, out_ref, total_ref,
-    full, ids, shares, hot, back, weight, rows, gate, up, hid, w_buf, d_buf, total, gate_grad, up_grad,
+    full, memo, memos, hot, back, weight, rows, gate, up, hid, w_buf, d_buf, total, gate_grad, up_grad,
     prow, came, acc, in_last, in_first, in_up, in_down, own_sem, w_sem, d_sem, note_send,
     note_recv, send_sem, recv_sem, twin_send, twin_recv, last_send, last_recv, first_send,
     first_recv, line_send, line_recv,
@@ -495,22 +495,27 @@
     ]
     for copy in own:
         copy.start()
-    ids[seat.expert] = ids_ref[...]
-    shares[seat.expert] = share_ref[...]
+    down_rows = lax.broadcasted_iota(jnp.int32, (tok, tok), 0)
+    over_columns = lax.broadcasted_iota(jnp.int32, (tok, tok), 1)
+    same = down_rows == over_columns
+    for n, ref in enumerate((ids_ref, share_ref)):
+        table = ref[...].astype(jnp.float32)
+        for choice in range(PAIR):
+            column = table[:, choice : choice + 1]
+            row = jnp.sum(jnp.where(same, column, 0.0), axis=0, keepdims=True)
+            memo[n * PAIR + choice : n * PAIR + choice + 1, :] = row
+    memo[2 * PAIR :, :] = jnp.zeros((memo.shape[0] - 2 * PAIR, tok), jnp.float32)
+    memos[seat.expert] = memo[...]
     seat.greet()
 
-    def note(n, ref, table, place, target):
+    peers = (seat.twin, seat.across_y, seat.corner)
+
+    def note(n, owner):
         return remote(
-            ref, table.at[seat.expert], note_send.at[n, place], note_recv.at[n, seat.expert], target
-        )
-
-    peers = (seat.twin, seat.across_y, seat.corner)
-    tables = ((ids_ref, ids), (share_ref, shares))
-    notes = [
-        note(n, ref, table, place, target)
-        for place, target in enumerate(peers)
-        for n, (ref, table) in enumerate(tables)
-    ]
+            memo, memos.at[owner], note_send.at[n], note_recv.at[owner], peers[n]
+        )
+
+    notes = [note(n, seat.expert) for n in range(len(peers))]
 
     def link(t, q, a, b, kind):
         d, beside = seat.spot(q, a, b)
@@ -542,10 +547,13 @@
 
     def early_line(k, _):
         q = seat.line(k)
-        pl.when(k > 0)(lambda: arrived(EARLY, q, 0, 0))
-        along(EARLY, q, 0, begin)
-        for kind in (FIRST, LAST, TWIN):
-            link(EARLY, q, 0, 0, kind).start()
+
+        @pl.when(k > 0)
+        def _():
+            arrived(EARLY, q, 0, 0)
+            along(EARLY, q, 0, begin)
+            for kind in (FIRST, LAST, TWIN):
+                link(EARLY, q, 0, 0, kind).start()
 
     def early_first(k, _):
         q = seat.line(k)
@@ -630,33 +638,27 @@
         copy.wait()
     for copy in notes:
         copy.start()
-    for kind in (FIRST, LAST, TWIN):
-        link(LATE, z, 0, 0, kind).start()
-    along(LATE, z, 0, begin)
+    for t in (EARLY, LATE):
+        along(t, z, 0, begin)
+        for kind in (FIRST, LAST, TWIN):
+            link(t, z, 0, 0, kind).start()
     for a in range(PAIR):
         for copy in load_up(0, a) + load_down(0, a):
             copy.start()
     for acts in (gate, up, hid, total):
         acts[...] = jnp.zeros_like(acts)
 
-    down_rows = lax.broadcasted_iota(jnp.int32, (tok, tok), 0)
-    over_columns = lax.broadcasted_iota(jnp.int32, (tok, tok), 1)
     before = (down_rows < over_columns).astype(jnp.bfloat16)
     slot_rows = lax.broadcasted_iota(jnp.int32, (slots, tok), 0).astype(jnp.float32)
     slot_columns = lax.broadcasted_iota(jnp.int32, (tok, slots), 1).astype(jnp.float32)
-    same = down_rows == over_columns
-    for target in peers:
-        other = target["expert"]
-        for n, (ref, table) in enumerate(tables):
-            remote(
-                ref, table.at[other], note_send.at[n, 0], note_recv.at[n, other], target
-            ).wait_recv()
+    mine = seat.expert.astype(jnp.float32)
+    for n, target in enumerate(peers):
+        note(n, target["expert"]).wait_recv()
     for block in range(blocks):
-        named = (ids[block] == seat.expert).astype(jnp.float32)
-        hit_column = jnp.sum(named, axis=1, keepdims=True)
-        share_column = jnp.sum(named * shares[block], axis=1, keepdims=True)
-        hit = jnp.sum(jnp.where(same, hit_column, 0.0), axis=0, keepdims=True)
-        share = jnp.sum(jnp.where(same, share_column, 0.0), axis=0, keepdims=True)
+        known = memos[block]
+        named = (known[0:PAIR] == mine).astype(jnp.float32)
+        hit = named[0:1] + named[1:2]
+        share = named[0:1] * known[2:3] + named[1:2] * known[3:4]
         earlier = jnp.dot(
             jnp.broadcast_to(hit, (8, tok)).astype(jnp.bfloat16), before,
             preferred_element_type=jnp.float32,
@@ -675,7 +677,7 @@
         depth, FRONT_PLAN,
         {
             "xl": early_line, "xa": early_first, "xb": from_last(EARLY), "gl": late_line,
-            "gb": from_last(LATE), "cx": g_products, "cg": x_products,
+            "gb": from_last(LATE), "cx": x_products, "cg": g_products,
         },
     )
 
@@ -903,8 +905,8 @@
         out_specs=(vmem, vmem),
         scratch_shapes=[
             pltpu.VMEM((2, shards, blocks) + piece, half),
-            pltpu.VMEM((blocks,) + expert_ids.shape, jnp.int32),
-            pltpu.VMEM((blocks,) + combine.shape, wide),
+            pltpu.VMEM((8, tok), wide),
+            pltpu.VMEM((blocks, 8, tok), wide),
             pltpu.VMEM((blocks, slots, tok), half),
             pltpu.VMEM((blocks, tok, slots), half),
             pltpu.VMEM((blocks, slots, 1), wide),
@@ -927,8 +929,8 @@
             dma((2,)),
             dma((PAIR, 2)),
             dma((PAIR,)),
-            dma((2, 3)),
-            dma((2, blocks)),
+            dma((3,)),
+            dma((blocks,)),
             dma((2, 5, depth * blocks)),
             dma((2, shards, blocks)),
             dma((shards, PAIR)),
@@ -1011,8 +1013,9 @@
         P("expert", "dp"),
     )
     count = mesh.shape["dp"]
-    if mesh.shape["expert"] == PAIR * PAIR and count % PAIR == 0 and count <= SHORT_RING:
-        body = functools.partial(local_cube, count // PAIR)
+    depth = 1 + max(k for _, k, _ in FRONT_PLAN)
+    if mesh.shape["expert"] == PAIR * PAIR and count == PAIR * depth:
+        body = functools.partial(local_cube, depth)
     else:
         body = functools.partial(local, ring_order(mesh))
     return jax.shard_map(

time: 149 us -> 137 us (0.919)
  Pallas kernels: 142 us -> 131 us
    pallas_call x1, Pallas kernels: 142 us -> 131 us  [cube(): pl.pallas_call(functools.partial(cube_kernel, depth, main), out_shape=(ja...]
where the time goes in v3:
time: 137 us
  Pallas kernels  131 us (96%)
  local copies, waits for them, and re-layouts  5.91 us (4%)
    pallas_call x1, Pallas kernels, cube(): pl.pallas_call(functools.partial(cube_kernel, depth, main), out_shape=(ja...  131 us
    unnamed x4, local copies, waits for them, and re-layouts  5.91 us

profile of v3, /device:TPU:0, one launch (start us, length us, event | category | flops | bytes accessed | tf_op | source)
XLA Modules:
  0.0 137.1 jit_solution(9281576755584962039)
XLA Ops:
  0.6 1.5 %copy.10.ids_ref = s32[256,2]{1,0:T(8,128)} copy(s32[256,2]{0,1:T(2,128)} %param.10) | data formatting | bytes 4096 | tf_op args[2]
  2.1 1.5 %copy.11.share_ref = f32[256,2]{1,0:T(8,128)} copy(f32[256,2]{0,1:T(2,128)} %param.11) | data formatting | bytes 4096 | tf_op args[3]
  3.6 130.6 %shard_map.95 = (bf16[256,512]{1,0:T(8,128)(2,1)}, f32[1,1792]{1,0:T(1,128)}) custom-call(s32[256,2]{1,0:T(8,128)} %copy.10.ids_ref, f32[256,2]{1,0:T(8,128)} %copy.11.share_ref, bf16[256,512]{1,0:T(8,128)(2,1)} %x_ref.1, bf16[256,512]{1,0:T(8,128)(2,1)} %g_ref.1, bf16[4096,1792]{1,0:T(8,128)(2,1)} %bitcast.3, bf16[4096,1792]{1,0:T(8,128)(2,1)} %bitcast.4, ...), custom_call_target="tpu_custom_call" | custom-call | tf_op jit(solution)/shard_map/pallas_call | solution.py:898
  134.2 1.7 %copy.14 = bf16[256,512]{1,0:T(8,128)(2,1)} copy(bf16[256,512]{1,0:T(8,128)(2,1)} %get-tuple-element.4) | data formatting | bytes 524288
  135.8 1.3 copy.15

commit v4 on v3

--- a/solution.py
+++ b/solution.py
@@ -377,7 +377,9 @@
         self.expert = lax.axis_index("expert")
         self.z, self.x = lax.div(self.dp, PAIR), lax.rem(self.dp, PAIR)
         self.y, self.core = lax.div(self.expert, PAIR), lax.rem(self.expert, PAIR)
-        self.table = [q for row in near_first(depth) for q in row]
+        self.order = [
+            lookup([row[k] for row in near_first(depth)], self.z) for k in range(depth)
+        ]
         core, dp, expert = self.core, self.dp, self.expert
         dx, dy = 1 - 2 * self.x, 2 - 4 * self.y
         self.twin = {"dp": dp, "expert": expert + 1 - 2 * core}
@@ -392,7 +394,10 @@
         self.has_down = self.z > 0
 
     def line(self, k):
-        return lookup(self.table, self.z * self.depth + k)
+        found = self.order[0]
+        for index in range(1, self.depth):
+            found = jnp.where(k == index, self.order[index], found)
+        return found
 
     def far(self, k):
         return self.line(self.depth - 1 - k)
@@ -434,19 +439,39 @@
 def run_plan(depth, plan, ops):
     names = sorted({(name, part) for name, _, part in plan})
     codes = [names.index((name, part)) * depth + k for name, k, part in plan]
+    base = 1 << (len(names) * depth - 1).bit_length()
+    group = 1
+    while base ** (group + 1) < 2**31 and group < 4:
+        group += 1
+    while len(codes) % group:
+        group -= 1
+    words = [
+        sum(code * base**n for n, code in enumerate(codes[i : i + group]))
+        for i in range(0, len(codes), group)
+    ]
+
+    def pick(which, k, low, high):
+        if high - low == 1:
+            name, part = names[low]
+            ops[name](k, part)
+            return
+        middle = (low + high) // 2
+        lax.cond(
+            which < middle,
+            lambda: pick(which, k, low, middle),
+            lambda: pick(which, k, middle, high),
+        )
 
     def turn(i, carry):
-        code = lookup(codes, i)
-        which, k = lax.div(code, depth), lax.rem(code, depth)
-        for index, (name, part) in enumerate(names):
-
-            @pl.when(which == index)
-            def _(name=name, part=part):
-                ops[name](k, part)
-
+        def one(_, word):
+            code = lax.rem(word, base)
+            pick(lax.div(code, depth), lax.rem(code, depth), 0, len(names))
+            return lax.div(word, base)
+
+        lax.fori_loop(0, group, one, lookup(words, i))
         return carry
 
-    lax.fori_loop(0, len(codes), turn, 0)
+    lax.fori_loop(0, len(words), turn, 0)
 
 
 def cube_kernel(

time: 137 us -> 135 us (0.985)
  Pallas kernels: 131 us -> 128 us
    pallas_call x1, Pallas kernels: 131 us -> 128 us  [cube(): pl.pallas_call(functools.partial(cube_kernel, depth, main), out_shape=(ja...]
where the time goes in v4:
time: 135 us
  Pallas kernels  128 us (95%)
  local copies, waits for them, and re-layouts  5.91 us (4%)
    pallas_call x1, Pallas kernels, cube(): pl.pallas_call(functools.partial(cube_kernel, depth, main), out_shape=(ja...  128 us
    unnamed x4, local copies, waits for them, and re-layouts  5.91 us

profile of v4, /device:TPU:0, one launch (start us, length us, event | category | flops | bytes accessed | tf_op | source)
XLA Modules:
  0.0 135.0 jit_solution(75303089740127200)
XLA Ops:
  0.6 1.5 %copy.10.ids_ref = s32[256,2]{1,0:T(8,128)} copy(s32[256,2]{0,1:T(2,128)} %param.10) | data formatting | bytes 4096 | tf_op args[2]
  2.1 1.5 %copy.11.share_ref = f32[256,2]{1,0:T(8,128)} copy(f32[256,2]{0,1:T(2,128)} %param.11) | data formatting | bytes 4096 | tf_op args[3]
  3.6 128.4 %shard_map.95 = (bf16[256,512]{1,0:T(8,128)(2,1)}, f32[1,1792]{1,0:T(1,128)}) custom-call(s32[256,2]{1,0:T(8,128)} %copy.10.ids_ref, f32[256,2]{1,0:T(8,128)} %copy.11.share_ref, bf16[256,512]{1,0:T(8,128)(2,1)} %x_ref.1, bf16[256,512]{1,0:T(8,128)(2,1)} %g_ref.1, bf16[4096,1792]{1,0:T(8,128)(2,1)} %bitcast.3, bf16[4096,1792]{1,0:T(8,128)(2,1)} %bitcast.4, ...), custom_call_target="tpu_custom_call" | custom-call | tf_op jit(solution)/shard_map/pallas_call | solution.py:923
  132.0 1.7 %copy.14 = bf16[256,512]{1,0:T(8,128)(2,1)} copy(bf16[256,512]{1,0:T(8,128)(2,1)} %get-tuple-element.4) | data formatting | bytes 524288
  133.7 1.3 copy.15
